TPU v7x, 128 devices: a whole 4x4x4 slice. The times are simulated.
128 devices in a mesh: rep: 1, r: 4 (over x), s: 32 (over y, z, core).
Axes of the slice: x: 4, y: 4, z: 4, core: 2. Of those that a mesh axis runs over, the one named last changes fastest.
Arguments:
- x: bfloat16 [128, 2048, 1024], P(('rep', 'r', 's'))
- dy: bfloat16 [128, 2048, 1024], P(('rep', 'r', 's'))
- w_gate: bfloat16 [2, 1024, 2560], P(None, 's')
- w_up: bfloat16 [2, 1024, 2560], P(None, 's')
- w_down: bfloat16 [2, 2560, 1024], P(None, 's')
Outputs:
- output 1: bfloat16 [128, 2048, 1024], P(('rep', 'r', 's'))
- output 2: bfloat16 [2, 1024, 2560], P('rep', 's')
- output 3: bfloat16 [2, 1024, 2560], P('rep', 's')
- output 4: bfloat16 [2, 2560, 1024], P('rep', 's')
All inputs are finite; a program needn't handle non-finite values.
Results may differ from a plain program's by a relative error of at most 0.018.
Values are sent between devices in bfloat16 or wider.
A program may use at most 1.5 GiB of HBM per device.

v0:
```python
import jax
import jax.numpy as jnp
from jax import lax
from jax.sharding import PartitionSpec as P

NAMES = ("w_gate", "w_up", "w_down")


def matmul(a, w):
    return jnp.dot(a, w, preferred_element_type=jnp.float32).astype(jnp.bfloat16)


def normed(h):
    wide = h.astype(jnp.float32)
    scale = lax.rsqrt(jnp.mean(wide**2, -1, keepdims=True) + 1e-6)
    return (wide * scale).astype(jnp.bfloat16)


def layer(h, w):
    a = normed(h)
    gate = jnp.dot(a, w["w_gate"], preferred_element_type=jnp.float32)
    up = jnp.dot(a, w["w_up"], preferred_element_type=jnp.float32)
    return h + matmul((jax.nn.silu(gate) * up).astype(jnp.bfloat16), w["w_down"])


def solution(mesh):
    def fetched(weights, number):
        return {name: lax.all_gather(w[number], "s", axis=0, tiled=True) for name, w in zip(NAMES, weights, strict=True)}

    def summed(term):
        return lax.psum(lax.psum_scatter(term, "s", scatter_dimension=0, tiled=True), "r")

    def step(x, dy, *weights):
        layers = weights[0].shape[0]
        h, inputs = x[0], []
        for number in range(layers):
            inputs.append(h)
            h = layer(h, fetched(weights, number))
        by_h, mine = dy[0], [None] * layers
        for number in reversed(range(layers)):
            _, back = jax.vjp(lambda w, h: layer(h, w), fetched(weights, number), inputs[number])
            by_w, by_h = back(by_h)
            mine[number] = [summed(by_w[name]) for name in NAMES]
        return (by_h[None], *(jnp.stack([mine[number][i] for number in range(layers)]) for i in range(3)))

    states, cut = P(("rep", "r", "s"), None, None), P(None, "s", None)
    return jax.shard_map(
        step,
        mesh=mesh,
        in_specs=(states, states) + (cut,) * 3,
        out_specs=(states,) + (P("rep", "s", None),) * 3,
        check_vma=False,
    )
```

profile of v0, /device:TPU:0, one launch (start us, length us, event | category | flops | bytes accessed | tf_op | source)
XLA Modules:
  0.0 942.6 jit_solution(14723788667721095755)
XLA Ops:
  31.1 29.7 %all-gather.13.cloned.1.call-done = bf16[1,1024,2560]{2,1,0:T(8,128)(2,1)} async-done(((bf16[1,32,2560]{2,1,0:T(8,128)(2,1)}), bf16[1,1024,2560]{2,1,0:T(8,128)(2,1)}) %all-gather.13.cloned.1.call-update) | async-done | bytes 5242896 | tf_op jit(solution)/shard_map/all_gather | solution.py:28
  60.8 18.3 %fusion.40 = f32[2048,2560]{1,0:T(8,128)} fusion(bf16[1,1024,2560]{2,1,0:T(8,128)(2,1)} %all-gather.13.cloned.1.call-done, bf16[1,2048,1024]{1,2,0:T(8,128)(2,1)} %copy.10, f32[2048]{0:T(1024)S(1)} %fusion.61), kind=kOutput, calls=%fused_computation.65 | convolution fusion | flops 10743709696 | bytes 30416896 | tf_op jit(solution)/shard_map/dot_general | solution.py:21
  79.1 30.5 %all-gather.15.cloned.1.call-done = bf16[1,1024,2560]{2,1,0:T(8,128)(2,1)} async-done(((bf16[1,32,2560]{2,1,0:T(8,128)(2,1)}), bf16[1,1024,2560]{2,1,0:T(8,128)(2,1)}) %all-gather.15.cloned.1.call-update) | async-done | bytes 5242896 | tf_op jit(solution)/shard_map/all_gather | solution.py:28
  109.6 28.8 %multiply_convert_fusion.1 = (bf16[2048,2560]{1,0:T(8,128)(2,1)}, f32[2048,2560]{1,0:T(8,128)}) fusion(f32[2048,2560]{1,0:T(8,128)} %fusion.40, bf16[1,1024,2560]{2,1,0:T(8,128)(2,1)} %all-gather.15.cloned.1.call-done, bf16[1,2048,1024]{1,2,0:T(8,128)(2,1)} %copy.10, f32[2048]{0:T(1024)S(1)} %fusion.61), kind=kOutput, calls=%fused_computation.13 | convolution fusion | flops 10775166976 | bytes 61874176 | tf_op jit(solution)/shard_map/dot_general | solution.py:22
  138.4 20.1 %all-gather.17.cloned.1.call-done = bf16[1,2560,1024]{2,1,0:T(8,128)(2,1)} async-done(((bf16[1,80,1024]{2,1,0:T(8,128)(2,1)}), bf16[1,2560,1024]{2,1,0:T(8,128)(2,1)}) %all-gather.17.cloned.1.call-update) | async-done | bytes 5242896 | tf_op jit(solution)/shard_map/all_gather | solution.py:28
  158.5 17.9 %fusion.18 = (f32[2048]{0:T(1024)S(1)}, bf16[2048,1024]{0,1:T(8,128)(2,1)}) fusion(bf16[2048,2560]{1,0:T(8,128)(2,1)} %get-tuple-element.20, bf16[1,2560,1024]{2,1,0:T(8,128)(2,1)} %all-gather.17.cloned.1.call-done, bf16[1,2048,1024]{1,2,0:T(8,128)(2,1)} %copy.10), kind=kOutput, calls=%fused_computation.40 | convolution fusion | flops 10747901952 | bytes 24125440 | tf_op jit(solution)/shard_map/dot_general | solution.py:10
  177.0 30.2 %all-gather.21.cloned.1.call-done = bf16[1,2560,1024]{2,1,0:T(8,128)(2,1)} async-done(((bf16[1,80,1024]{2,1,0:T(8,128)(2,1)}), bf16[1,2560,1024]{2,1,0:T(8,128)(2,1)}) %all-gather.21.cloned.1.call-update) | async-done | bytes 5242896 | tf_op jit(solution)/shard_map/all_gather | solution.py:28
  224.2 32.4 %all-gather.23.cloned.1.call-done = bf16[1,1024,2560]{2,1,0:T(8,128)(2,1)} async-done(((bf16[1,32,2560]{2,1,0:T(8,128)(2,1)}), bf16[1,1024,2560]{2,1,0:T(8,128)(2,1)}) %all-gather.23.cloned.1.call-update) | async-done | bytes 5242896 | tf_op jit(solution)/shard_map/all_gather | solution.py:28
  256.5 18.3 %fusion.24 = f32[2048,2560]{1,0:T(8,128)} fusion(bf16[1,1024,2560]{2,1,0:T(8,128)(2,1)} %all-gather.23.cloned.1.call-done, bf16[2048,1024]{0,1:T(8,128)(2,1)} %get-tuple-element.23, f32[2048]{0:T(1024)S(1)} %fusion.62), kind=kOutput, calls=%fused_computation.49 | convolution fusion | flops 10743709696 | bytes 30416896 | tf_op jit(solution)/shard_map/jvp()/dot_general | solution.py:22
  274.8 31.0 %all-gather.19.cloned.1.call-done = bf16[1,1024,2560]{2,1,0:T(8,128)(2,1)} async-done(((bf16[1,32,2560]{2,1,0:T(8,128)(2,1)}), bf16[1,1024,2560]{2,1,0:T(8,128)(2,1)}) %all-gather.19.cloned.1.call-update) | async-done | bytes 5242896 | tf_op jit(solution)/shard_map/all_gather | solution.py:28
  305.8 32.3 %fusion.1 = (bf16[2048,2560]{1,0:T(8,128)(2,1)}, f32[2048,2560]{1,0:T(8,128)}) fusion(f32[2048,2560]{1,0:T(8,128)} %fusion.24, bf16[2048,2560]{1,0:T(8,128)(2,1)} %convolution_convert_fusion.1, bf16[1,1024,2560]{2,1,0:T(8,128)(2,1)} %all-gather.19.cloned.1.call-done, bf16[2048,1024]{0,1:T(8,128)(2,1)} %get-tuple-element.23, f32[2048]{0:T(1024)S(1)} %fusion.62), kind=kOutput, calls=%fused_computation.7 | convolution fusion | flops 10806624256 | bytes 72359936 | tf_op jit(solution)/shard_map/jvp()/dot_general | solution.py:21
  338.1 22.0 %fusion.21 = bf16[2560,1024]{1,0:T(8,128)(2,1)} fusion(f32[2048,2560]{1,0:T(8,128)} %fusion.24, bf16[1,2048,1024]{2,1,0:T(8,128)(2,1)} %param.6, f32[2048,2560]{1,0:T(8,128)} %get-tuple-element.25), kind=kOutput, calls=%fused_computation.43 | convolution fusion | flops 10771496960 | bytes 51380224 | tf_op jit(solution)/shard_map/transpose(jvp())/dot_general | solution.py:10
  360.2 20.2 %fusion.7 = bf16[2048,1024]{0,1:T(8,128)(2,1)} fusion(bf16[2048,2560]{1,0:T(8,128)(2,1)} %convolution_convert_fusion.1, bf16[1,1024,2560]{2,1,0:T(8,128)(2,1)} %all-gather.23.cloned.1.call-done, f32[2048,2560]{1,0:T(8,128)} %get-tuple-element.25), kind=kOutput, calls=%fused_computation.25 | convolution fusion | flops 10768875520 | bytes 40894464 | tf_op jit(solution)/shard_map/transpose(jvp())/dot_general | solution.py:22
  380.5 17.5 %fusion.20 = (f32[2048]{0:T(1024)S(1)}, bf16[2048,1024]{0,1:T(8,128)(2,1)S(1)}) fusion(bf16[2048,1024]{0,1:T(8,128)(2,1)} %get-tuple-element.23, bf16[2048,1024]{0,1:T(8,128)(2,1)} %fusion.7, bf16[2048,2560]{1,0:T(8,128)(2,1)} %get-tuple-element.24, bf16[1,1024,2560]{2,1,0:T(8,128)(2,1)} %all-gather.19.cloned.1.call-done), kind=kOutput, calls=%fused_computation.42 | convolution fusion | flops 10747901952 | bytes 28319744 | tf_op jit(solution)/shard_map/transpose(jvp())/dot_general | solution.py:21
  419.4 31.5 %fusion.3 = (bf16[2048,2560]{1,0:T(8,128)(2,1)}, bf16[2048,2560]{1,0:T(8,128)(2,1)}) fusion(f32[2048,2560]{1,0:T(8,128)} %fusion.40, f32[2048,2560]{1,0:T(8,128)} %get-tuple-element.21, bf16[2048,1024]{0,1:T(8,128)(2,1)} %copy-done, bf16[1,2560,1024]{2,1,0:T(8,128)(2,1)} %all-gather.17.cloned.1.call-done), kind=kOutput, calls=%fused_computation.9 | convolution fusion | flops 10805575680 | bytes 72351744 | tf_op jit(solution)/shard_map/transpose(jvp())/dot_general | solution.py:10
  450.9 20.1 %fusion.22 = bf16[1024,2560]{1,0:T(8,128)(2,1)} fusion(bf16[2048,2560]{1,0:T(8,128)(2,1)} %get-tuple-element.29, bf16[1,2048,1024]{1,2,0:T(8,128)(2,1)} %copy.10, f32[2048]{0:T(1024)S(1)} %copy-done.6, f32[2048,2560]{1,0:T(8,128)} %fusion.40), kind=kOutput, calls=%fused_computation.44 | convolution fusion | flops 10777788416 | bytes 40902656 | tf_op jit(solution)/shard_map/transpose(jvp())/dot_general | solution.py:22
  471.1 20.5 %fusion.23 = bf16[1024,2560]{1,0:T(8,128)(2,1)} fusion(bf16[2048,2560]{1,0:T(8,128)(2,1)} %convolution_convert_fusion.1, bf16[2048,1024]{0,1:T(8,128)(2,1)} %get-tuple-element.23, f32[2048]{0:T(1024)S(1)} %copy-done.8, f32[2048,2560]{1,0:T(8,128)} %get-tuple-element.25), kind=kOutput, calls=%fused_computation.45 | convolution fusion | flops 10777788416 | bytes 40902656 | tf_op jit(solution)/shard_map/transpose(jvp())/dot_general | solution.py:22
  524.9 20.0 %fusion.9 = bf16[2048,1024]{0,1:T(8,128)(2,1)} fusion(bf16[2048,2560]{1,0:T(8,128)(2,1)} %get-tuple-element.29, bf16[1,1024,2560]{2,1,0:T(8,128)(2,1)} %all-gather.15.cloned.1.call-done, f32[2048,2560]{1,0:T(8,128)} %fusion.40), kind=kOutput, calls=%fused_computation.27 | convolution fusion | flops 10768875520 | bytes 40894464 | tf_op jit(solution)/shard_map/transpose(jvp())/dot_general | solution.py:22
  544.9 18.7 %fusion.17 = (f32[2048]{0:T(1024)S(1)}, bf16[2048,1024]{0,1:T(8,128)(2,1)}) fusion(bf16[1,2048,1024]{1,2,0:T(8,128)(2,1)} %copy.10, bf16[2048,1024]{0,1:T(8,128)(2,1)} %fusion.9, bf16[2048,2560]{1,0:T(8,128)(2,1)} %get-tuple-element.28, bf16[1,1024,2560]{2,1,0:T(8,128)(2,1)} %all-gather.13.cloned.1.call-done), kind=kOutput, calls=%fused_computation.39 | convolution fusion | flops 10747901952 | bytes 28319744 | tf_op jit(solution)/shard_map/transpose(jvp())/dot_general | solution.py:21
  563.6 56.9 %reduce-scatter.11.cloned.1.call-done = bf16[32,2560]{1,0:T(8,128)(2,1)} async-done(((bf16[1024,2560]{1,0:T(8,128)(2,1)}), bf16[32,2560]{1,0:T(8,128)(2,1)}) %reduce-scatter.11.cloned.1.call-update) | async-done | bytes 163856 | tf_op jit(solution)/shard_map/reduce_scatter | solution.py:31
  620.6 87.9 %reduce-scatter.13.cloned.1.call-done = bf16[32,2560]{1,0:T(8,128)(2,1)} async-done(((bf16[1024,2560]{1,0:T(8,128)(2,1)}), bf16[32,2560]{1,0:T(8,128)(2,1)}) %reduce-scatter.13.cloned.1.call-update) | async-done | bytes 163856 | tf_op jit(solution)/shard_map/reduce_scatter | solution.py:31
  708.5 88.1 %reduce-scatter.9.cloned.1.call-done = bf16[32,2560]{1,0:T(8,128)(2,1)} async-done(((bf16[1024,2560]{1,0:T(8,128)(2,1)}), bf16[32,2560]{1,0:T(8,128)(2,1)}) %reduce-scatter.9.cloned.1.call-update) | async-done | bytes 163856 | tf_op jit(solution)/shard_map/reduce_scatter | solution.py:31
  796.5 87.9 %reduce-scatter.7.cloned.1.call-done = bf16[32,2560]{1,0:T(8,128)(2,1)} async-done(((bf16[1024,2560]{1,0:T(8,128)(2,1)}), bf16[32,2560]{1,0:T(8,128)(2,1)}) %reduce-scatter.7.cloned.1.call-update) | async-done | bytes 163856 | tf_op jit(solution)/shard_map/reduce_scatter | solution.py:31
  898.5 33.5 %all-reduce.3.cloned.1.call-done = (bf16[1,32,2560]{2,1,0:T(8,128)(2,1)}, bf16[1,32,2560]{2,1,0:T(8,128)(2,1)}, bf16[1,32,2560]{2,1,0:T(8,128)(2,1)}, bf16[1,32,...) async-done(((bf16[1,32,2560]{2,1,0:T(8,128)(2,1)}, bf16[1,32,2560]{2,1,0:T(8,128)(2,1)}, bf16[1,32,2560]{2,1,0:T(8,128)(2,1)}, ...) | async-done | bytes 983056 | tf_op jit(solution)/shard_map/psum | solution.py:31
  (69 shorter events, 113.8 us)
Async XLA Ops:
  7.2 53.6 %all-gather.13.cloned.1.call-start = ((), (), s32[]{:S(2)}) async-start(), calls=%async_computation.12 | async-start | bytes 5406720 | tf_op jit(solution)/shard_map/all_gather | solution.py:28
  9.0 100.7 %all-gather.15.cloned.1.call-start = ((), (), s32[]{:S(2)}) async-start(), calls=%async_computation.13 | async-start | bytes 5406720 | tf_op jit(solution)/shard_map/all_gather | solution.py:28
  10.8 147.7 %all-gather.17.cloned.1.call-start = ((), (), s32[]{:S(2)}) async-start(), calls=%async_computation.14 | async-start | bytes 5406720 | tf_op jit(solution)/shard_map/all_gather | solution.py:28
  12.6 194.6 %all-gather.21.cloned.1.call-start = ((), (), s32[]{:S(2)}) async-start(), calls=%async_computation.16 | async-start | bytes 5406720 | tf_op jit(solution)/shard_map/all_gather | solution.py:28
  13.2 243.3 %all-gather.23.cloned.1.call-start = ((), (), s32[]{:S(2)}) async-start(), calls=%async_computation.17 | async-start | bytes 5406720 | tf_op jit(solution)/shard_map/all_gather | solution.py:28
  13.8 292.0 %all-gather.19.cloned.1.call-start = ((), (), s32[]{:S(2)}) async-start(), calls=%async_computation.15 | async-start | bytes 5406720 | tf_op jit(solution)/shard_map/all_gather | solution.py:28
  14.4 549.3 %reduce-scatter.17.cloned.1.call-start = ((), (), s32[]{:S(2)}) async-start(), calls=%async_computation.11 | async-start | bytes 5406720 | tf_op jit(solution)/shard_map/reduce_scatter | solution.py:31
  23.9 0.6 copy-start.3
  24.5 85.1 %copy-start.5 = (f32[2048]{0:T(1024)}, f32[2048]{0:T(1024)S(1)}, u32[]{:S(2)}) copy-start(f32[2048]{0:T(1024)S(1)} %fusion.61) | copy-start | bytes 24580
  176.4 0.6 copy-start.9
  177.0 221.0 %copy-start.7 = (f32[2048]{0:T(1024)}, f32[2048]{0:T(1024)S(1)}, u32[]{:S(2)}) copy-start(f32[2048]{0:T(1024)S(1)} %fusion.62) | copy-start | bytes 24580
  360.2 203.5 %reduce-scatter.15.cloned.1.call-start = ((), (), s32[]{:S(2)}) async-start(), calls=%async_computation.10 | async-start | bytes 5406720 | tf_op jit(solution)/shard_map/reduce_scatter | solution.py:31
  380.5 17.5 %copy-start.10 = (f32[2048]{0:T(1024)S(1)}, f32[2048]{0:T(1024)}, u32[]{:S(2)}) copy-start(f32[2048]{0:T(1024)} %copy-done.9) | copy-start | bytes 24580
  380.5 17.6 %copy-start.1 = (bf16[1,2048,1024]{1,2,0:T(8,128)(2,1)S(1)}, bf16[1,2048,1024]{1,2,0:T(8,128)(2,1)}, u32[]{:S(2)}) copy-start(bf16[1,2048,1024]{1,2,0:T(8,128)(2,1)} %copy.9) | copy-start | bytes 12582916
  380.5 17.6 %copy-start.2 = (bf16[2048,1024]{0,1:T(8,128)(2,1)S(1)}, bf16[2048,1024]{0,1:T(8,128)(2,1)}, u32[]{:S(2)}) copy-start(bf16[2048,1024]{0,1:T(8,128)(2,1)} %get-tuple-element.23) | copy-start | bytes 12582916
  401.6 2.0 copy-start
  419.3 201.3 %reduce-scatter.11.cloned.1.call-start = ((), (), s32[]{:S(2)}) async-start(), calls=%async_computation.8 | async-start | bytes 5406720 | tf_op jit(solution)/shard_map/reduce_scatter | solution.py:31
  419.4 31.6 %copy-start.6 = (f32[2048]{0:T(1024)S(1)}, f32[2048]{0:T(1024)}, u32[]{:S(2)}) copy-start(f32[2048]{0:T(1024)} %copy-done.5) | copy-start | bytes 24580
  450.9 20.2 %copy-start.8 = (f32[2048]{0:T(1024)S(1)}, f32[2048]{0:T(1024)}, u32[]{:S(2)}) copy-start(f32[2048]{0:T(1024)} %copy-done.7) | copy-start | bytes 24580
  471.1 237.4 %reduce-scatter.13.cloned.1.call-start = ((), (), s32[]{:S(2)}) async-start(), calls=%async_computation.9 | async-start | bytes 5406720 | tf_op jit(solution)/shard_map/reduce_scatter | solution.py:31
  491.7 304.9 %reduce-scatter.9.cloned.1.call-start = ((), (), s32[]{:S(2)}) async-start(), calls=%async_computation.7 | async-start | bytes 5406720 | tf_op jit(solution)/shard_map/reduce_scatter | solution.py:31
  508.2 376.2 %reduce-scatter.7.cloned.1.call-start = ((), (), s32[]{:S(2)}) async-start(), calls=%async_computation.6 | async-start | bytes 5406720 | tf_op jit(solution)/shard_map/reduce_scatter | solution.py:31
  524.9 407.2 %all-reduce.3.cloned.1.call-start = ((), (), s32[]{:S(2)}) async-start(), calls=%async_computation.18 | async-start | bytes 1966080 | tf_op jit(solution)/shard_map/psum | solution.py:31
  544.9 339.6 %copy-start.4 = (f32[2048]{0:T(1024)S(1)}, f32[2048]{0:T(1024)}, u32[]{:S(2)}) copy-start(f32[2048]{0:T(1024)} %copy-done.3) | copy-start | bytes 24580
Sparse Core Ops, SparseCore 0:
  10.8 49.9 all-gather.12
  63.0 46.5 all-gather.14
  111.9 46.5 all-gather.16
  160.6 46.5 all-gather.20
  209.9 46.5 all-gather.22
  259.2 46.5 all-gather.18
  360.3 84.1 reduce-scatter.16
  448.3 84.2 reduce-scatter.14
  536.3 84.2 reduce-scatter.10
  624.1 84.2 reduce-scatter.12
  712.2 84.2 reduce-scatter.8
  800.1 84.2 reduce-scatter.6
  887.2 44.8 all-reduce.2
where the time goes:
time: 949 us; the launch traced here: 943 us
  waiting for transfers between devices  530 us (56%)
  matrix products  352 us (37%)
  local copies, waits for them, and re-layouts  27.8 us (3%)
  other arithmetic  18.1 us (2%)
  between operations  14.2 us (1%)
    reduce_scatter x6, waiting for transfers between devices, summed(): lax.psum_scatter(term, 's', scatter_dimension=0, tiled=True)  321 us
    all_gather x6, waiting for transfers between devices, fetched(): lax.all_gather(w[number], 's', axis=0, tiled=True)  174 us
    dot_general x6, matrix products, layer(): up = jnp.dot(a, w['w_up'], preferred_element_type=jnp.float32)  128 us
    dot_general x6, matrix products, layer(): gate = jnp.dot(a, w['w_gate'], preferred_element_type=jnp.float32)  120 us
    dot_general x5, matrix products, matmul(): jnp.dot(a, w, preferred_element_type=jnp.float32).astype(jnp.bfloat16)  104 us
    psum x1, waiting for transfers between devices, summed(): lax.psum(lax.psum_scatter(term, 's', scatter_dimension=0, tiled=True), 'r')  33.5 us
    unnamed x25, local copies, waits for them, and re-layouts  22.6 us
  transfers between devices with their start and end apart: 13, of which 11 were waited for; matrix products, arithmetic and copies ran while one was open for 36% of the time, Pallas kernels for 0%

commit v1 on v0

v1 whole, which is shorter than its diff:
```python
import functools

import jax
import jax.numpy as jnp
from jax import lax
from jax.experimental import pallas as pl
from jax.experimental.pallas import tpu as pltpu
from jax.sharding import PartitionSpec as P

F32, BF16 = jnp.float32, jnp.bfloat16
MESH = pl.DeviceIdType.MESH
ANY = pl.BlockSpec(memory_space=pl.ANY)
LIMIT = 60 * 1024 * 1024
SIZE = {"x": 4, "y": 4, "z": 4, "c": 2}


def here():
    s = lax.axis_index("s")
    return {"x": lax.axis_index("r"), "y": lax.div(s, 8), "z": lax.rem(lax.div(s, 2), 4), "c": lax.rem(s, 2)}


def moved(p, axis, step):
    return {**p, axis: lax.rem(p[axis] + step, SIZE[axis])}


def device(p):
    return {"r": p["x"], "s": (p["y"] * 4 + p["z"]) * 2 + p["c"]}


def greet(peers):
    me = here()
    barrier = pltpu.get_barrier_semaphore()
    for axis, step in peers:
        pl.semaphore_signal(barrier, inc=1, device_id=device(moved(me, axis, step)), device_id_type=MESH)
    pl.semaphore_wait(barrier, len(peers))


class Wires:
    def __init__(self, send, recv):
        self.send, self.recv, self.pending = send, recv, []

    def go(self, i, src, dst, to):
        copy = lambda: pltpu.make_async_remote_copy(src, dst, self.send.at[i], self.recv.at[i], device_id=device(to), device_id_type=MESH)
        copy().start()

    def sent(self, i, src, to):
        pltpu.make_async_remote_copy(src, src, self.send.at[i], self.recv.at[i], device_id=device(to), device_id_type=MESH).wait_send()

    def wait(self, i, dst, to):
        pltpu.make_async_remote_copy(dst, dst, self.send.at[i], self.recv.at[i], device_id=device(to), device_id_type=MESH).wait_recv()


GATHER_PEERS = (("c", 1), ("y", 1), ("y", 3), ("z", 1), ("z", 3))
GATHER_SEMS = 12


def gather_stages(first, second, w, full, local, send, recv):
    wires = Wires(send, recv)
    half = w.shape[-1] // 2
    left, right = pl.ds(0, half), pl.ds(half, half)

    def block(p, **free):
        p = {**p, **free}
        return full.at[p["y"], p["z"], p["c"]]

    def row(p, cols=None):
        p = {**p, first: slice(None)}
        return full.at[p["y"], p["z"], p["c"]] if cols is None else full.at[p["y"], p["z"], p["c"], :, cols]

    def part(p, cols):
        return full.at[p["y"], p["z"], p["c"], :, cols]

    def s0():
        me = here()
        pltpu.make_async_copy(w, block(me), local).start()
        wires.go(0, w, block(me), moved(me, first, 1))
        wires.go(1, w, block(me), moved(me, first, 3))

    def s1():
        me = here()
        before, after = moved(me, first, 3), moved(me, first, 1)
        wires.wait(0, block(before), before)
        wires.go(2, part(before, left), part(before, left), after)
        wires.wait(1, block(after), after)
        wires.go(3, part(after, right), part(after, right), before)
        pltpu.make_async_copy(w, block(me), local).wait()

    def s2():
        me = here()
        far = moved(me, first, 2)
        wires.wait(2, part(far, left), me)
        wires.wait(3, part(far, right), me)
        for i, (axis, step) in ((4, (second, 1)), (5, (second, 3)), (8, ("c", 1))):
            wires.go(i, row(me), row(me), moved(me, axis, step))

    def s3():
        me = here()
        before, after, mate = moved(me, second, 3), moved(me, second, 1), moved(me, "c", 1)
        wires.wait(4, row(before), before)
        wires.go(6, row(before, left), row(before, left), after)
        wires.wait(5, row(after), after)
        wires.go(7, row(after, right), row(after, right), before)
        wires.go(9, row(before), row(before), mate)
        wires.go(10, row(after), row(after), mate)

    def s4():
        me = here()
        far, mate = moved(me, second, 2), moved(me, "c", 1)
        wires.wait(6, row(far, left), me)
        wires.wait(7, row(far, right), me)
        wires.go(11, row(far), row(far), mate)

    def s5():
        me = here()
        mate = moved(me, "c", 1)
        for i, step in ((8, 0), (9, 3), (10, 1), (11, 2)):
            wires.wait(i, row(moved(mate, second, step)), me)
        for i in (0, 1):
            wires.sent(i, w, me)
        for i, cols in ((2, left), (3, right)):
            wires.sent(i, part(me, cols), me)
        for i in (4, 5, 8, 9, 10, 11):
            wires.sent(i, row(me), me)
        for i, cols in ((6, left), (7, right)):
            wires.sent(i, row(me, cols), me)

    return [s0, s1, s2, s3, s4, s5]


def gather_scratch(n):
    return [pltpu.SemaphoreType.DMA((n,)), pltpu.SemaphoreType.DMA((n, GATHER_SEMS)), pltpu.SemaphoreType.DMA((n, GATHER_SEMS))]


GATHER_ORDERS = (("z", "y"), ("y", "z"), ("z", "y"))


def gather_plan(ws, fulls, scratch):
    local, send, recv = scratch
    lists = [
        gather_stages(*GATHER_ORDERS[i % 3], w, full, local.at[i], send.at[i], recv.at[i])
        for i, (w, full) in enumerate(zip(ws, fulls, strict=True))
    ]
    return [[stages[k] for stages in lists] for k in range(len(lists[0]))]


def blocks_of(w):
    return (4, 4, 2, w.shape[0], w.shape[1])


def gather(ws, collective_id):
    n = len(ws)

    def kernel(*refs):
        plan = gather_plan(refs[:n], refs[n : 2 * n], refs[2 * n :])
        greet(GATHER_PEERS)
        for steps in plan:
            for step in steps:
                step()

    fulls = pl.pallas_call(
        kernel,
        out_shape=[jax.ShapeDtypeStruct(blocks_of(w), BF16) for w in ws],
        in_specs=[pl.BlockSpec(memory_space=pltpu.VMEM)] * n,
        out_specs=[ANY] * n,
        scratch_shapes=gather_scratch(n),
        compiler_params=pltpu.CompilerParams(collective_id=collective_id, has_side_effects=True),
        name="gather",
    )(*ws)
    return [f.reshape(-1, f.shape[-1]) for f in fulls]


SUM_PEERS = (("c", 1), *((axis, step) for axis in "xyz" for step in (1, 2, 3)))
SUM_SEMS = 18
SUM_ORDERS = ("xyz", "yzx", "zxy")


def sum_scratch(rows, columns):
    w = columns // 4
    vm = lambda *shape: pltpu.VMEM((*shape, rows, w), BF16)
    wide = lambda *shape: pltpu.VMEM((*shape, rows, w), F32)
    return [
        vm(4, 4, 4), vm(4, 4, 4),
        vm(2, 8), vm(2, 8), vm(2, 16), vm(2, 16), wide(16),
        vm(2, 2), vm(2, 2), vm(2, 4), vm(2, 4), wide(4),
        vm(3), vm(3), vm(4),
        pltpu.SemaphoreType.DMA((8,)), pltpu.SemaphoreType.DMA((SUM_SEMS,)), pltpu.SemaphoreType.DMA((SUM_SEMS,)),
    ]


SUM_REFS = 18


def sum_stages(order, term, out, refs):
    own, mates, o1, i1, o2, i2, k1, o3, i3, o4, i4, k2, o5, i5, ob, local, send, recv = refs
    wires = Wires(send, recv)
    A, B, D = order
    w = own.shape[-1]

    def at(**p):
        return p["y"], p["z"], p["x"]

    def chip(p):
        return own[at(**p)].astype(F32) + mates[at(**p)].astype(F32)

    def fetch(me, q):
        return pltpu.make_async_copy(term.at[:, :, me["c"], :, pl.ds(q * w, w)], own.at[:, :, q], local.at[q])

    def r0():
        me = here()
        mate = moved(me, "c", 1)
        for q in range(4):
            wires.go(q, term.at[:, :, mate["c"], :, pl.ds(q * w, w)], mates.at[:, :, q], mate)
            fetch(me, q).start()

    def r1():
        me = here()
        for q in range(4):
            fetch(me, q).wait()
            wires.wait(q, mates.at[:, :, q], me)
        far = lax.rem(me[A] + 2, 4)
        for turn, step in ((0, 1), (1, 3)):

            @pl.loop(0, 8)
            def _(i):
                b, d = lax.div(i, 4), lax.rem(i, 4)
                o1[turn, i] = chip({A: far, B: 2 * turn + b, D: d}).astype(BF16)

            wires.go(4 + turn, o1.at[turn], i1.at[turn], moved(me, A, step))

    def r2():
        me = here()
        for turn, step in ((0, 1), (1, 3)):
            wires.wait(4 + turn, i1.at[turn], me)
            to = moved(me, A, step)

            @pl.loop(0, 8)
            def _(i):
                b, d = lax.div(i, 4), lax.rem(i, 4)
                o2[turn, 8 * turn + i] = (chip({A: to[A], B: 2 * turn + b, D: d}) + i1[turn, i].astype(F32)).astype(BF16)
                o2[turn, 8 * (1 - turn) + i] = chip({A: to[A], B: 2 * (1 - turn) + b, D: d}).astype(BF16)

            wires.go(6 + turn, o2.at[turn], i2.at[turn], to)

    def r3():
        me = here()
        for turn in (0, 1):
            wires.wait(6 + turn, i2.at[turn], me)

        @pl.loop(0, 16)
        def _(i):
            k1[i] = chip({A: me[A], B: lax.div(i, 4), D: lax.rem(i, 4)}) + i2[0, i].astype(F32) + i2[1, i].astype(F32)

        far = lax.rem(me[B] + 2, 4)
        for turn, step in ((0, 1), (1, 3)):
            for d in range(2):
                o3[turn, d] = k1[far * 4 + 2 * turn + d].astype(BF16)
            wires.go(8 + turn, o3.at[turn], i3.at[turn], moved(me, B, step))

    def r4():
        me = here()
        for turn, step in ((0, 1), (1, 3)):
            wires.wait(8 + turn, i3.at[turn], me)
            to = moved(me, B, step)
            for d in range(2):
                o4[turn, 2 * turn + d] = (k1[to[B] * 4 + 2 * turn + d] + i3[turn, d].astype(F32)).astype(BF16)
                o4[turn, 2 * (1 - turn) + d] = k1[to[B] * 4 + 2 * (1 - turn) + d].astype(BF16)
            wires.go(10 + turn, o4.at[turn], i4.at[turn], to)

    def r5():
        me = here()
        for turn in (0, 1):
            wires.wait(10 + turn, i4.at[turn], me)
        for d in range(4):
            k2[d] = k1[me[B] * 4 + d] + i4[0, d].astype(F32) + i4[1, d].astype(F32)
        for j in (1, 2, 3):
            to = moved(me, D, j)
            o5[j - 1] = k2[to[D]].astype(BF16)
            wires.go(11 + j, o5.at[j - 1], i5.at[j - 1], to)

    def r6():
        me = here()
        total = k2[me[D]]
        for j in (1, 2, 3):
            wires.wait(11 + j, i5.at[j - 1], me)
            total = total + i5[j - 1].astype(F32)
        ob[me["x"]] = total.astype(BF16)
        for j in (1, 2, 3):
            wires.go(14 + j, ob.at[me["x"]], ob.at[me["x"]], moved(me, "x", j))

    def put(q):
        return pltpu.make_async_copy(ob.at[q], out.at[:, pl.ds(q * w, w)], local.at[4 + q])

    def r7():
        me = here()
        for j in (1, 2, 3):
            wires.wait(14 + j, ob.at[moved(me, "x", 4 - j)["x"]], me)
        for q in range(4):
            put(q).start()
        for q in range(4):
            wires.sent(q, mates.at[:, :, q], me)
        for turn in (0, 1):
            wires.sent(4 + turn, o1.at[turn], me)
            wires.sent(6 + turn, o2.at[turn], me)
            wires.sent(8 + turn, o3.at[turn], me)
            wires.sent(10 + turn, o4.at[turn], me)
        for j in (1, 2, 3):
            wires.sent(11 + j, o5.at[j - 1], me)
            wires.sent(14 + j, ob.at[me["x"]], me)
        for q in range(4):
            put(q).wait()

    return [r0, r1, r2, r3, r4, r5, r6, r7]


def sum_plan(terms, outs, scratch):
    lists = [sum_stages(SUM_ORDERS[i], terms[i], outs[i], scratch[SUM_REFS * i : SUM_REFS * (i + 1)]) for i in range(len(terms))]
    return [[stages[k] for stages in lists] for k in range(len(lists[0]))]


def cut(term):
    return term.reshape(4, 4, 2, term.shape[0] // 32, term.shape[1])


def summed(terms, collective_id):
    n = len(terms)
    terms = [cut(t) for t in terms]

    def kernel(*refs):
        plan = sum_plan(refs[:n], refs[n : 2 * n], refs[2 * n :])
        greet(SUM_PEERS)
        for steps in plan:
            for step in steps:
                step()

    return pl.pallas_call(
        kernel,
        out_shape=[jax.ShapeDtypeStruct(t.shape[3:], BF16) for t in terms],
        in_specs=[ANY] * n,
        out_specs=[ANY] * n,
        scratch_shapes=[s for t in terms for s in sum_scratch(*t.shape[3:])],
        compiler_params=pltpu.CompilerParams(collective_id=collective_id, has_side_effects=True, vmem_limit_bytes=LIMIT),
        name="summed",
    )(*terms)


def dot(a, b, dims=((1,), (0,))):
    return lax.dot_general(a, b, (dims, ((), ())), preferred_element_type=F32)


def scale_of(wide):
    return lax.rsqrt(jnp.mean(wide * wide, -1, keepdims=True) + 1e-6)


def norm_into(h, a, at, chunk=512):
    @pl.loop(0, h.shape[0], step=chunk)
    def _(m):
        rows = pl.ds(m, chunk)
        wide = h[rows, :].astype(F32)
        value = (wide * scale_of(wide)).astype(BF16)
        if a is not None:
            a[rows, :] = value
        if at is not None:
            at[:, rows] = value.T


def whole(shape):
    return pl.BlockSpec(shape, lambda i: (0,) * len(shape), pipeline_mode=pl.Buffered(1))


TILE, CHUNK = 256, 512


def forward(h, wg, wu, wd):
    tokens, d = h.shape
    ff = wg.shape[1]
    steps = ff // TILE

    def kernel(h_ref, wg_ref, wu_ref, wd_ref, y_ref, g_ref, u_ref, at_ref, a, acc):
        i = pl.program_id(0)

        @pl.when(i == 0)
        def _():
            norm_into(h_ref, a, at_ref)
            acc[...] = jnp.zeros_like(acc)

        @pl.loop(0, tokens, step=CHUNK)
        def _(m):
            rows = pl.ds(m, CHUNK)
            g = dot(a[rows, :], wg_ref[...])
            u = dot(a[rows, :], wu_ref[...])
            g_ref[rows, :] = g
            u_ref[rows, :] = u
            act = (g * jax.nn.sigmoid(g) * u).astype(BF16)
            acc[rows, :] += dot(act, wd_ref[...])

        @pl.when(i == steps - 1)
        def _():
            y_ref[...] = h_ref[...] + acc[...].astype(BF16)

    across = pl.BlockSpec((d, TILE), lambda i: (0, i))
    tile = pl.BlockSpec((tokens, TILE), lambda i: (0, i))
    return pl.pallas_call(
        kernel,
        grid=(steps,),
        out_shape=[
            jax.ShapeDtypeStruct(h.shape, BF16),
            jax.ShapeDtypeStruct((tokens, ff), F32),
            jax.ShapeDtypeStruct((tokens, ff), F32),
            jax.ShapeDtypeStruct((d, tokens), BF16),
        ],
        in_specs=[whole(h.shape), across, across, pl.BlockSpec((TILE, d), lambda i: (i, 0))],
        out_specs=[whole(h.shape), tile, tile, whole((d, tokens))],
        scratch_shapes=[pltpu.VMEM(h.shape, BF16), pltpu.VMEM(h.shape, F32)],
        compiler_params=pltpu.CompilerParams(vmem_limit_bytes=LIMIT),
        name="forward",
    )(h, wg, wu, wd)


def hidden_grads(g, u, by_act):
    sig = jax.nn.sigmoid(g)
    silu = g * sig
    by_act = by_act.astype(BF16).astype(F32)
    return (silu * u).astype(BF16), (by_act * u * (sig * (1 + g * (1 - sig)))).astype(BF16), (by_act * silu).astype(BF16)


def backward_hidden(by_y, wd, saved=None, fresh=None):
    tokens, d = by_y.shape
    ff = wd.shape[0]
    steps = ff // TILE

    def kernel(*refs):
        i = pl.program_id(0)
        if fresh is not None:
            h_ref, wg_ref, wu_ref, by_ref, wd_ref, dg_ref, du_ref, dwg_ref, dwu_ref, dwd_ref, act, a, at = refs

            @pl.when(i == 0)
            def _():
                norm_into(h_ref, a, at)
        else:
            at, g_ref, u_ref, by_ref, wd_ref, dg_ref, du_ref, dwg_ref, dwu_ref, dwd_ref, act = refs

        @pl.loop(0, tokens, step=CHUNK)
        def _(m):
            rows = pl.ds(m, CHUNK)
            if fresh is not None:
                g, u = dot(a[rows, :], wg_ref[...]), dot(a[rows, :], wu_ref[...])
            else:
                g, u = g_ref[rows, :], u_ref[rows, :]
            by_act = dot(by_ref[rows, :], wd_ref[...], ((1,), (1,)))
            act[rows, :], dg_ref[rows, :], du_ref[rows, :] = hidden_grads(g, u, by_act)

        dwd_ref[...] = dot(act[...], by_ref[...], ((0,), (0,))).astype(BF16)
        dwg_ref[...] = dot(at[...], dg_ref[...]).astype(BF16)
        dwu_ref[...] = dot(at[...], du_ref[...]).astype(BF16)

    across = pl.BlockSpec((d, TILE), lambda i: (0, i))
    down = pl.BlockSpec((TILE, d), lambda i: (i, 0))
    tile = pl.BlockSpec((tokens, TILE), lambda i: (0, i))
    scratch = [pltpu.VMEM((tokens, TILE), BF16)]
    if fresh is not None:
        specs = [whole((tokens, d)), across, across]
        scratch += [pltpu.VMEM((tokens, d), BF16), pltpu.VMEM((d, tokens), BF16)]
    else:
        specs = [whole((d, tokens)), tile, tile]
    return pl.pallas_call(
        kernel,
        grid=(steps,),
        out_shape=[jax.ShapeDtypeStruct((tokens, ff), BF16)] * 2 + [jax.ShapeDtypeStruct((d, ff), BF16)] * 2 + [jax.ShapeDtypeStruct((ff, d), BF16)],
        in_specs=specs + [whole((tokens, d)), down],
        out_specs=[tile, tile, across, across, down],
        scratch_shapes=scratch,
        compiler_params=pltpu.CompilerParams(vmem_limit_bytes=LIMIT),
        name="backward_hidden",
    )(*(fresh if fresh is not None else saved), by_y, wd)


def backward_input(dg, du, wg, wu, h, by_y):
    tokens, d = h.shape
    ff = dg.shape[1]
    chunk = 256

    def kernel(dg_ref, du_ref, wg_ref, wu_ref, h_ref, by_ref, out_ref):
        by_a = dot(dg_ref[...], wg_ref[...], ((1,), (1,))) + dot(du_ref[...], wu_ref[...], ((1,), (1,)))
        by_a = by_a.astype(BF16).astype(F32)
        wide = h_ref[...].astype(F32)
        scale = scale_of(wide)
        back = jnp.sum(by_a * wide, -1, keepdims=True) * (scale * scale * scale) * (1 / d)
        out_ref[...] = by_ref[...] + (by_a * scale - wide * back).astype(BF16)

    rows = lambda n: pl.BlockSpec((chunk, n), lambda i: (i, 0))
    return pl.pallas_call(
        kernel,
        grid=(tokens // chunk,),
        out_shape=jax.ShapeDtypeStruct(h.shape, BF16),
        in_specs=[rows(ff), rows(ff), whole(wg.shape), whole(wu.shape), rows(d), rows(d)],
        out_specs=rows(d),
        compiler_params=pltpu.CompilerParams(vmem_limit_bytes=LIMIT),
        name="backward_input",
    )(dg, du, wg, wu, h, by_y)


def solution(mesh):
    def step(x, dy, *weights):
        x, dy = x[0], dy[0]
        w0 = gather([w[0] for w in weights], 1)
        w1 = gather([w[1] for w in weights], 1)
        h1, g0, u0, at0 = forward(x, *w0)
        dg1, du1, *terms1 = backward_hidden(dy, w1[2], fresh=(h1, w1[0], w1[1]))
        by_h1 = backward_input(dg1, du1, w1[0], w1[1], h1, dy)
        dg0, du0, *terms0 = backward_hidden(by_h1, w0[2], saved=(at0, g0, u0))
        by_x = backward_input(dg0, du0, w0[0], w0[1], x, by_h1)
        sums1 = summed(terms1, 2)
        sums0 = summed(terms0, 2)
        return (by_x[None], *(jnp.stack([sums0[i], sums1[i]]) for i in range(3)))

    states, shard = P(("rep", "r", "s"), None, None), P(None, "s", None)
    return jax.shard_map(
        step,
        mesh=mesh,
        in_specs=(states, states) + (shard,) * 3,
        out_specs=(states,) + (P("rep", "s", None),) * 3,
        check_vma=False,
    )
```

time: 949 us -> 520 us (0.55)
  waiting for transfers between devices: 530 us -> 0 us
  Pallas kernels: 0 us -> 510 us
  matrix products: 352 us -> 0 us
  local copies, waits for them, and re-layouts: 27.8 us -> 3.75 us
  between operations: 14.2 us -> 0.7 us
  other arithmetic: 18.1 us -> 5.01 us
    pallas_call x0 -> x9, Pallas kernels: none -> 510 us  [the longest x2 147 us: backward_hidden(): pl.pallas_call(kernel, grid=(steps,), out_shape=[jax.ShapeDtypeStruct((to...]
    dot_general x17 -> x0, matrix products: 352 us -> none  [the longest x6 128 us: layer(): up = jnp.dot(a, w['w_up'], preferred_element_type=jnp.float32)]
    reduce_scatter x6 -> x0, waiting for transfers between devices: 321 us -> none  [summed(): lax.psum_scatter(term, 's', scatter_dimension=0, tiled=True)]
    all_gather x6 -> x0, waiting for transfers between devices: 174 us -> none  [fetched(): lax.all_gather(w[number], 's', axis=0, tiled=True)]
    psum x1 -> x0, waiting for transfers between devices: 33.5 us -> none  [summed(): lax.psum(lax.psum_scatter(term, 's', scatter_dimension=0, tiled=True), 'r')]
    unnamed x25 -> x6, local copies, waits for them, and re-layouts: 22.6 us -> 0.01 us
  transfers between devices with their start and end apart: 13 -> 0, of which waited for: 11 -> 0; matrix products, arithmetic and copies ran while one was open for 36% -> 0% of each run, Pallas kernels for 0% -> 0%
where the time goes in v1:
time: 520 us
  Pallas kernels  510 us (98%)
    pallas_call x2, Pallas kernels, backward_hidden(): pl.pallas_call(kernel, grid=(steps,), out_shape=[jax.ShapeDtypeStruct((to...  147 us
    pallas_call x2, Pallas kernels, gather(): pl.pallas_call(kernel, out_shape=[jax.ShapeDtypeStruct(blocks_of(w), BF16...  126 us
    pallas_call x2, Pallas kernels, summed(): pl.pallas_call(kernel, out_shape=[jax.ShapeDtypeStruct(t.shape[3:], BF16)...  124 us
    pallas_call x2, Pallas kernels, backward_input(): pl.pallas_call(kernel, grid=(tokens // chunk,), out_shape=jax.ShapeDtypeS...  63 us
    pallas_call x1, Pallas kernels, forward(): pl.pallas_call(kernel, grid=(steps,), out_shape=[jax.ShapeDtypeStruct(h.s...  51 us

profile of v1, /device:TPU:0, one launch (start us, length us, event | category | flops | bytes accessed | tf_op | source)
XLA Modules:
  0.0 519.9 jit_solution(10142923419483105581)
XLA Ops:
  0.6 1.8 slice_bitcast_fusion
  2.4 2.0 slice_bitcast_fusion.1
  4.4 63.7 %gather.3 = (bf16[4,4,2,32,2560]{4,3,2,1,0:T(8,128)(2,1)}, bf16[4,4,2,32,2560]{4,3,2,1,0:T(8,128)(2,1)}, bf16[4,4,2,80,1024]{4,3,2,1,0:T(8,128)(2,1)}) custom-call(bf16[32,2560]{1,0:T(8,128)(2,1)} %get-tuple-element.63.refs_0_, bf16[32,2560]{1,0:T(8,128)(2,1)} %get-tuple-element.58.refs_1_, bf16[80,1024]{1,0:T(8,128)(2,1)} %get-tuple-element.56.refs_2_), custom_call_target="tpu_custom_call" | custom-call | tf_op jit(solution)/shard_map/gather/pallas_call | solution.py:160
  68.1 61.9 %gather.2 = (bf16[4,4,2,32,2560]{4,3,2,1,0:T(8,128)(2,1)}, bf16[4,4,2,32,2560]{4,3,2,1,0:T(8,128)(2,1)}, bf16[4,4,2,80,1024]{4,3,2,1,0:T(8,128)(2,1)}) custom-call(bf16[32,2560]{1,0:T(8,128)(2,1)} %get-tuple-element.62.refs_0_, bf16[32,2560]{1,0:T(8,128)(2,1)} %get-tuple-element.59.refs_1_, bf16[80,1024]{1,0:T(8,128)(2,1)} %get-tuple-element.57.refs_2_), custom_call_target="tpu_custom_call" | custom-call | tf_op jit(solution)/shard_map/gather/pallas_call | solution.py:160
  130.0 51.0 %forward.1 = (bf16[2048,1024]{1,0:T(8,128)(2,1)}, f32[2048,2560]{1,0:T(8,128)}, f32[2048,2560]{1,0:T(8,128)}, bf16[1024,2048]{1,0:T(8,128)(2,1)}) custom-call(bf16[2048,1024]{1,0:T(8,128)(2,1)} %bitcast.43, bf16[1024,2560]{1,0:T(8,128)(2,1)} %bitcast.33, bf16[1024,2560]{1,0:T(8,128)(2,1)} %bitcast.35, bf16[2560,1024]{1,0:T(8,128)(2,1)} %bitcast.37), custom_call_target="tpu_custom_call" | custom-call | tf_op jit(solution)/shard_map/forward/pallas_call | solution.py:402
  181.0 83.4 %backward_hidden.2 = (bf16[2048,2560]{1,0:T(8,128)(2,1)}, bf16[2048,2560]{1,0:T(8,128)(2,1)}, bf16[1024,2560]{1,0:T(8,128)(2,1)}, bf16[1024,2560]{1,0:T(8,128)(2,1)}, bf16[2560,1024]{1,0:T(8,128)(2,1)}) custom-call(bf16[2048,1024]{1,0:T(8,128)(2,1)} %get-tuple-element.36.refs_0_.h_ref, bf16[1024,2560]{1,0:T(8,128)(2,1)} %bitcast.39, ...), custom_call_target="tpu_custom_call" | custom-call | tf_op jit(solution)/shard_map/backward_hidden/pallas_call | solution.py:465
  264.4 31.4 %backward_input.2.refs_3_.by_ref = bf16[2048,1024]{1,0:T(8,128)(2,1)} custom-call(bf16[2048,2560]{1,0:T(8,128)(2,1)} %get-tuple-element.40.dg_ref, bf16[2048,2560]{1,0:T(8,128)(2,1)} %get-tuple-element.41.du_ref, bf16[1024,2560]{1,0:T(8,128)(2,1)} %bitcast.40, bf16[1024,2560]{1,0:T(8,128)(2,1)} %bitcast.42, ...), custom_call_target="tpu_custom_call" | custom-call | tf_op jit(solution)/shard_map/backward_input/pallas_call | solution.py:491
  295.8 63.7 %backward_hidden.3 = (bf16[2048,2560]{1,0:T(8,128)(2,1)}, bf16[2048,2560]{1,0:T(8,128)(2,1)}, bf16[1024,2560]{1,0:T(8,128)(2,1)}, bf16[1024,2560]{1,0:T(8,128)(2,1)}, bf16[2560,1024]{1,0:T(8,128)(2,1)}) custom-call(bf16[1024,2048]{1,0:T(8,128)(2,1)} %get-tuple-element.33.refs_0_, f32[2048,2560]{1,0:T(8,128)} %get-tuple-element.34.refs_1_, ...), custom_call_target="tpu_custom_call" | custom-call | tf_op jit(solution)/shard_map/backward_hidden/pallas_call | solution.py:465
  359.6 31.6 %backward_input.3 = bf16[2048,1024]{1,0:T(8,128)(2,1)} custom-call(bf16[2048,2560]{1,0:T(8,128)(2,1)} %get-tuple-element.42.dg_ref, bf16[2048,2560]{1,0:T(8,128)(2,1)} %get-tuple-element.43.du_ref, bf16[1024,2560]{1,0:T(8,128)(2,1)} %bitcast.34, bf16[1024,2560]{1,0:T(8,128)(2,1)} %bitcast.36, bf16[2048,1024]{1,0:T(8,128)(2,1)} %bitcast.44, ...), custom_call_target="tpu_custom_call" | custom-call | tf_op jit(solution)/shard_map/backward_input/pallas_call | solution.py:491
  391.1 62.4 %summed.2 = (bf16[32,2560]{1,0:T(8,128)(2,1)}, bf16[32,2560]{1,0:T(8,128)(2,1)}, bf16[80,1024]{1,0:T(8,128)(2,1)}) custom-call(bf16[4,4,2,32,2560]{4,3,2,1,0:T(8,128)(2,1)} %bitcast.51, bf16[4,4,2,32,2560]{4,3,2,1,0:T(8,128)(2,1)} %bitcast.52, bf16[4,4,2,80,1024]{4,3,2,1,0:T(8,128)(2,1)} %bitcast.53), custom_call_target="tpu_custom_call" | custom-call | tf_op jit(solution)/shard_map/summed/pallas_call | solution.py:335
  453.5 0.0 copy-start.2
  453.5 0.0 copy-start.1
  453.6 0.0 copy-start
  453.6 61.3 %summed.3 = (bf16[32,2560]{1,0:T(8,128)(2,1)}, bf16[32,2560]{1,0:T(8,128)(2,1)}, bf16[80,1024]{1,0:T(8,128)(2,1)}) custom-call(bf16[4,4,2,32,2560]{4,3,2,1,0:T(8,128)(2,1)} %bitcast.47, bf16[4,4,2,32,2560]{4,3,2,1,0:T(8,128)(2,1)} %bitcast.48, bf16[4,4,2,80,1024]{4,3,2,1,0:T(8,128)(2,1)} %bitcast.49), custom_call_target="tpu_custom_call" | custom-call | tf_op jit(solution)/shard_map/summed/pallas_call | solution.py:335
  514.9 0.0 copy-done.2
  514.9 1.7 pad_maximum_fusion
  516.6 0.0 copy-done.1
  516.6 1.7 pad_maximum_fusion.1
  518.3 0.0 copy-done
  518.3 1.7 pad_maximum_fusion.2
Async XLA Ops:
  453.5 61.4 %copy-start.2 = (bf16[32,2560]{1,0:T(8,128)(2,1)S(1)}, bf16[32,2560]{1,0:T(8,128)(2,1)}, u32[]{:S(2)}) copy-start(bf16[32,2560]{1,0:T(8,128)(2,1)} %get-tuple-element.47) | copy-start | bytes 491524
  453.5 63.1 %copy-start.1 = (bf16[32,2560]{1,0:T(8,128)(2,1)S(1)}, bf16[32,2560]{1,0:T(8,128)(2,1)}, u32[]{:S(2)}) copy-start(bf16[32,2560]{1,0:T(8,128)(2,1)} %get-tuple-element.52) | copy-start | bytes 491524
  453.6 64.7 %copy-start = (bf16[80,1024]{1,0:T(8,128)(2,1)S(1)}, bf16[80,1024]{1,0:T(8,128)(2,1)}, u32[]{:S(2)}) copy-start(bf16[80,1024]{1,0:T(8,128)(2,1)} %get-tuple-element.54) | copy-start | bytes 491524

commit v2 on v1

v2 whole, which is shorter than its diff:
```python
import functools

import jax
import jax.numpy as jnp
from jax import lax
from jax.experimental import pallas as pl
from jax.experimental.pallas import tpu as pltpu
from jax.sharding import PartitionSpec as P

F32, BF16 = jnp.float32, jnp.bfloat16
MESH = pl.DeviceIdType.MESH
ANY = pl.BlockSpec(memory_space=pl.ANY)
LIMIT = 66_000_000
SIZE = {"x": 4, "y": 4, "z": 4, "c": 2}


def here():
    s = lax.axis_index("s")
    return {"x": lax.axis_index("r"), "y": lax.div(s, 8), "z": lax.rem(lax.div(s, 2), 4), "c": lax.rem(s, 2)}


def moved(p, axis, step):
    return {**p, axis: lax.rem(p[axis] + step, SIZE[axis])}


def device(p):
    return {"r": p["x"], "s": (p["y"] * 4 + p["z"]) * 2 + p["c"]}


def greet(peers):
    me = here()
    barrier = pltpu.get_barrier_semaphore()
    for peer in peers:
        to = me
        for axis, step in peer if isinstance(peer[0], tuple) else (peer,):
            to = moved(to, axis, step)
        pl.semaphore_signal(barrier, inc=1, device_id=device(to), device_id_type=MESH)
    pl.semaphore_wait(barrier, len(peers))


class Wires:
    def __init__(self, send, recv):
        self.send, self.recv, self.pending = send, recv, []

    def go(self, i, src, dst, to):
        copy = lambda: pltpu.make_async_remote_copy(src, dst, self.send.at[i], self.recv.at[i], device_id=device(to), device_id_type=MESH)
        copy().start()

    def sent(self, i, src, to):
        pltpu.make_async_remote_copy(src, src, self.send.at[i], self.recv.at[i], device_id=device(to), device_id_type=MESH).wait_send()

    def wait(self, i, dst, to):
        pltpu.make_async_remote_copy(dst, dst, self.send.at[i], self.recv.at[i], device_id=device(to), device_id_type=MESH).wait_recv()


def gather_stages(first, second, w, full, local, send, recv):
    wires = Wires(send, recv)
    half = w.shape[-1] // 2
    left, right = pl.ds(0, half), pl.ds(half, half)

    def block(p, **free):
        p = {**p, **free}
        return full.at[p["y"], p["z"], p["c"]]

    def row(p, cols=None):
        p = {**p, first: slice(None)}
        return full.at[p["y"], p["z"], p["c"]] if cols is None else full.at[p["y"], p["z"], p["c"], :, cols]

    def part(p, cols):
        return full.at[p["y"], p["z"], p["c"], :, cols]

    def s0():
        me = here()
        pltpu.make_async_copy(w, block(me), local).start()
        wires.go(0, w, block(me), moved(me, first, 1))
        wires.go(1, w, block(me), moved(me, first, 3))

    def s1():
        me = here()
        before, after = moved(me, first, 3), moved(me, first, 1)
        wires.wait(0, block(before), before)
        wires.go(2, part(before, left), part(before, left), after)
        wires.wait(1, block(after), after)
        wires.go(3, part(after, right), part(after, right), before)
        pltpu.make_async_copy(w, block(me), local).wait()

    def s2():
        me = here()
        far = moved(me, first, 2)
        wires.wait(2, part(far, left), me)
        wires.wait(3, part(far, right), me)
        for i, (axis, step) in ((4, (second, 1)), (5, (second, 3)), (8, ("c", 1))):
            wires.go(i, row(me), row(me), moved(me, axis, step))

    def s3():
        me = here()
        before, after, mate = moved(me, second, 3), moved(me, second, 1), moved(me, "c", 1)
        wires.wait(4, row(before), before)
        wires.go(6, row(before, left), row(before, left), after)
        wires.wait(5, row(after), after)
        wires.go(7, row(after, right), row(after, right), before)
        wires.go(9, row(before), row(before), mate)
        wires.go(10, row(after), row(after), mate)

    def s4():
        me = here()
        far, mate = moved(me, second, 2), moved(me, "c", 1)
        wires.wait(6, row(far, left), me)
        wires.wait(7, row(far, right), me)
        wires.go(11, row(far), row(far), mate)

    def s5():
        me = here()
        mate = moved(me, "c", 1)
        for i, step in ((8, 0), (9, 3), (10, 1), (11, 2)):
            wires.wait(i, row(moved(mate, second, step)), me)
        for i in (0, 1):
            wires.sent(i, w, me)
        for i, cols in ((2, left), (3, right)):
            wires.sent(i, part(me, cols), me)
        for i in (4, 5, 8, 9, 10, 11):
            wires.sent(i, row(me), me)
        for i, cols in ((6, left), (7, right)):
            wires.sent(i, row(me, cols), me)

    return [s0, s1, s2, s3, s4, s5]


def gather_stages_x(first, second, w, full, local, send, recv):
    wires = Wires(send, recv)
    quarter = w.shape[-1] // 4
    half = quarter // 2

    def cols(q, at=0, size=quarter):
        return pl.ds(pl.multiple_of(q * quarter + at, half), size)

    def part(p, c, **free):
        p = {**p, **free}
        return full.at[p["y"], p["z"], p["c"], :, c]

    def row(p, c):
        return part(p, c, **{first: slice(None)})

    def plane(p, q, ys=slice(None)):
        return full.at[ys, :, p["c"], :, cols(q)]

    def halves(me):
        return cols(me["x"], 0, half), cols(me["x"], half, half)

    def s0():
        me = here()
        q = cols(me["x"])
        pltpu.make_async_copy(w.at[:, q], part(me, q), local).start()
        wires.go(0, w.at[:, q], part(me, q), moved(me, first, 1))
        wires.go(1, w.at[:, q], part(me, q), moved(me, first, 3))

    def s1():
        me = here()
        q, (left, right) = cols(me["x"]), halves(me)
        before, after = moved(me, first, 3), moved(me, first, 1)
        wires.wait(0, part(before, q), before)
        wires.go(2, part(before, left), part(before, left), after)
        wires.wait(1, part(after, q), after)
        wires.go(3, part(after, right), part(after, right), before)
        pltpu.make_async_copy(w.at[:, q], part(me, q), local).wait()

    def s2():
        me = here()
        q, (left, right) = cols(me["x"]), halves(me)
        far = moved(me, first, 2)
        wires.wait(2, part(far, left), me)
        wires.wait(3, part(far, right), me)
        wires.go(4, row(me, q), row(me, q), moved(me, second, 1))
        wires.go(5, row(me, q), row(me, q), moved(me, second, 3))

    def s3():
        me = here()
        q, (left, right) = cols(me["x"]), halves(me)
        before, after = moved(me, second, 3), moved(me, second, 1)
        wires.wait(4, row(before, q), before)
        wires.go(6, row(before, left), row(before, left), after)
        wires.wait(5, row(after, q), after)
        wires.go(7, row(after, right), row(after, right), before)

    def s4():
        me = here()
        left, right = halves(me)
        far = moved(me, second, 2)
        wires.wait(6, row(far, left), me)
        wires.wait(7, row(far, right), me)
        q = me["x"]
        for i, (axis, step) in ((8, ("x", 1)), (9, ("x", 3)), (12, ("c", 1))):
            wires.go(i, plane(me, q), plane(me, q), moved(me, axis, step))

    low, high = slice(0, 2), slice(2, 4)

    def s5():
        me = here()
        before, after, mate = moved(me, "x", 3), moved(me, "x", 1), moved(me, "c", 1)
        wires.wait(8, plane(me, before["x"]), me)
        wires.go(10, plane(me, before["x"], low), plane(me, before["x"], low), after)
        wires.wait(9, plane(me, after["x"]), me)
        wires.go(11, plane(me, after["x"], high), plane(me, after["x"], high), before)
        wires.go(13, plane(me, before["x"]), plane(me, before["x"]), mate)
        wires.go(14, plane(me, after["x"]), plane(me, after["x"]), mate)

    def s6():
        me = here()
        far, mate = moved(me, "x", 2)["x"], moved(me, "c", 1)
        wires.wait(10, plane(me, far, low), me)
        wires.wait(11, plane(me, far, high), me)
        wires.go(15, plane(me, far), plane(me, far), mate)

    def s7():
        me = here()
        mate = moved(me, "c", 1)
        q, (left, right) = cols(me["x"]), halves(me)
        for i, step in ((12, 0), (13, 3), (14, 1), (15, 2)):
            wires.wait(i, plane(mate, moved(me, "x", step)["x"]), me)
        for i in (0, 1):
            wires.sent(i, w.at[:, q], me)
        for i, c in ((2, left), (3, right)):
            wires.sent(i, part(me, c), me)
        for i, c in ((4, q), (5, q), (6, left), (7, right)):
            wires.sent(i, row(me, c), me)
        for i in (8, 9, 12, 13, 14, 15):
            wires.sent(i, plane(me, me["x"]), me)
        for i, ys in ((10, low), (11, high)):
            wires.sent(i, plane(me, me["x"], ys), me)

    return [s0, s1, s2, s3, s4, s5, s6, s7]


def gather_stages_direct(w, full, local, send, recv, start, size):
    wires = Wires(send, recv)
    cols = pl.ds(start, size)
    others = [(j, k) for j in (1, 3, 0, 2) for k in (1, 3, 0, 2) if (j, k) != (0, 0)]

    def part(p):
        return full.at[p["y"], p["z"], p["c"], :, cols]

    def every(c):
        return full.at[:, :, c, :, cols]

    def s0():
        me = here()
        for n, (j, k) in enumerate(others):
            wires.go(n, w.at[:, cols], part(me), moved(moved(me, "y", j), "z", k))
        pltpu.make_async_copy(w.at[:, cols], part(me), local).start()

    def s1():
        me = here()
        pltpu.make_async_copy(w.at[:, cols], part(me), local).wait()
        for n, (j, k) in enumerate(others):
            wires.wait(n, part(moved(moved(me, "y", 4 - j), "z", 4 - k)), me)
        wires.go(15, every(me["c"]), every(me["c"]), moved(me, "c", 1))

    def s2():
        wires.wait(15, every(moved(here(), "c", 1)["c"]), here())

    def s3():
        me = here()
        for n in range(15):
            wires.sent(n, w.at[:, cols], me)
        wires.sent(15, every(me["c"]), me)

    return [s0, s1, s2, s3]


def blocks_of(w):
    return (4, 4, 2, w.shape[0], w.shape[1])


PLANE_PEERS = (("c", 1), ("x", 1), ("x", 3), *((("y", j), ("z", k)) for j in range(4) for k in range(4) if j or k))


class Exchange:
    def before(self):
        greet(self.peers)

    def grid_step(self, plan, marks, i):
        for at, steps in marks.items():
            if at != "end":

                @pl.when(i == at)
                def _():
                    if at == 0:
                        self.before()
                    for which, number in steps:
                        plan[which][number]()

    def finish(self, plan, marks):
        for which, number in marks["end"]:
            plan[which][number]()


class Gather(Exchange):
    peers = (("c", 1), *((axis, step) for axis in "yz" for step in (1, 2, 3)), ("x", 1), ("x", 3))

    def __init__(self, ws):
        n = len(ws)
        self.operands = list(ws)
        self.in_specs = [pl.BlockSpec(memory_space=pltpu.VMEM)] * n
        self.out_shape = [jax.ShapeDtypeStruct(blocks_of(w), BF16) for w in ws]
        self.out_specs = [ANY] * n
        sems = [12, 12, 16]
        self.scratch = [pltpu.SemaphoreType.DMA((n,))] + [pltpu.SemaphoreType.DMA((k,)) for k in sems for _ in range(2)]

    def plan(self, ins, outs, scratch):
        local, *sems = scratch
        makers = (functools.partial(gather_stages, "z", "y"), functools.partial(gather_stages, "y", "z"), functools.partial(gather_stages_x, "z", "y"))
        return [make(w, full, local.at[i], sems[2 * i], sems[2 * i + 1]) for i, (make, w, full) in enumerate(zip(makers, ins, outs, strict=True))]

    @staticmethod
    def whole_matrices(fulls):
        return [f.reshape(-1, f.shape[-1]) for f in fulls]


def gather_stages_chunk(first, second, w, full, local, send, recv, start, size, to=None):
    wires = Wires(send, recv)
    to = start if to is None else to
    source = w.at[:, pl.ds(start, size)]
    cols, left, right = pl.ds(to, size), pl.ds(to, size // 2), pl.ds(to + size // 2, size // 2)

    def part(p, c):
        return full.at[p["y"], p["z"], p["c"], :, c]

    def row(p, c):
        return part({**p, first: slice(None)}, c)

    def s0():
        me = here()
        for j in (1, 3, 2):
            wires.go(j - 1, source, part(me, cols), moved(me, first, j))
        pltpu.make_async_copy(source, part(me, cols), local).start()

    def s1():
        me = here()
        pltpu.make_async_copy(source, part(me, cols), local).wait()
        for j in (1, 3, 2):
            wires.wait(j - 1, part(moved(me, first, 4 - j), cols), me)
        wires.go(3, row(me, cols), row(me, cols), moved(me, second, 1))
        wires.go(4, row(me, cols), row(me, cols), moved(me, second, 3))

    def s2():
        me = here()
        before, after = moved(me, second, 3), moved(me, second, 1)
        wires.wait(3, row(before, cols), me)
        wires.go(5, row(before, left), row(before, left), after)
        wires.wait(4, row(after, cols), me)
        wires.go(6, row(after, right), row(after, right), before)

    def every(c):
        return full.at[:, :, c, :, cols]

    def s3():
        me = here()
        far, mate = moved(me, second, 2), moved(me, "c", 1)
        wires.wait(5, row(far, left), me)
        wires.wait(6, row(far, right), me)
        wires.go(7, every(me["c"]), every(me["c"]), mate)

    def s4():
        me = here()
        wires.wait(7, every(moved(me, "c", 1)["c"]), me)

    def s5():
        me = here()
        for j in range(3):
            wires.sent(j, source, me)
        for i, c in ((3, cols), (4, cols), (5, left), (6, right)):
            wires.sent(i, row(me, c), me)
        wires.sent(7, every(me["c"]), me)

    return [s0, s1, s2, s3, s4, s5]


SUM_PEERS = (("c", 1), *((axis, step) for axis in "xyz" for step in (1, 2, 3)))
SUM_SEMS = 20
SUM_ORDERS = ("xyz", "yzx", "zxy")


def sum_scratch(rows, columns):
    w = columns // 4
    vm = lambda *shape: pltpu.VMEM((*shape, rows, w), BF16)
    wide = lambda *shape: pltpu.VMEM((*shape, rows, w), F32)
    return [
        *[pltpu.VMEM((4, 4, rows, columns), BF16)] * 2,
        vm(2, 8), vm(2, 8), vm(2, 16), vm(2, 16), wide(16),
        vm(2, 2), vm(2, 2), vm(2, 4), vm(2, 4), wide(4),
        vm(3), vm(3), vm(4),
        pltpu.SemaphoreType.DMA((12,)), pltpu.SemaphoreType.DMA((SUM_SEMS,)), pltpu.SemaphoreType.DMA((SUM_SEMS,)),
    ]


SUM_REFS = 18


def sum_stages(order, term, there, out, refs):
    own, mates, o1, i1, o2, i2, k1, o3, i3, o4, i4, k2, o5, i5, ob, local, send, recv = refs
    wires = Wires(send, recv)
    A, B, D = order
    w = out.shape[-1] // 4

    def lane(q):
        return pl.ds(pl.multiple_of(q * w, 128), w)

    def chip(p):
        at = p["y"], p["z"], slice(None), lane(p["x"])
        return own[at].astype(F32) + mates[at].astype(F32)

    QUARTERS = (2, 1, 3, 0)

    def quarter(ref, me, k, core=None):
        n = lax.rem(me[A] + QUARTERS[k], 4)
        y, z, x = (n if A == axis else slice(None) for axis in "yzx")
        cols = lane(n) if A == "x" else slice(None)
        return ref.at[y, z, :, cols] if core is None else ref.at[y, z, core, :, cols]

    def fetch(me, k):
        return pltpu.make_async_copy(quarter(term, me, k, me["c"]), quarter(own, me, k), local.at[k])

    def fetch_mates(me, k):
        return pltpu.make_async_copy(quarter(there, me, k), quarter(mates, me, k), local.at[8 + k])

    def r0():
        me = here()
        mate = moved(me, "c", 1)
        for k in range(4):
            if there is None:
                wires.go(k, quarter(term, me, k, mate["c"]), quarter(mates, me, k), mate)
            else:
                fetch_mates(me, k).start()
            fetch(me, k).start()

    def have(me, k):
        fetch(me, k).wait()
        if there is None:
            wires.wait(k, quarter(mates, me, k), me)
        else:
            fetch_mates(me, k).wait()

    def r1():
        me = here()
        have(me, 0)
        far = lax.rem(me[A] + 2, 4)
        for turn, step in ((0, 1), (1, 3)):

            @pl.loop(0, 8)
            def _(i):
                b, d = lax.div(i, 4), lax.rem(i, 4)
                o1[turn, i] = chip({A: far, B: 2 * turn + b, D: d}).astype(BF16)

            wires.go(4 + turn, o1.at[turn], i1.at[turn], moved(me, A, step))
        for turn, step in ((0, 1), (1, 3)):
            to = moved(me, A, step)
            have(me, 1 + turn)

            @pl.loop(0, 8)
            def _(i):
                b, d = lax.div(i, 4), lax.rem(i, 4)
                o2[turn, 8 * (1 - turn) + i] = chip({A: to[A], B: 2 * (1 - turn) + b, D: d}).astype(BF16)

            rest = pl.ds(8 * (1 - turn), 8)
            wires.go(18 + turn, o2.at[turn, rest], i2.at[turn, rest], to)

    def r2():
        me = here()
        for turn, step in ((0, 1), (1, 3)):
            wires.wait(4 + turn, i1.at[turn], me)
            to = moved(me, A, step)

            @pl.loop(0, 8)
            def _(i):
                b, d = lax.div(i, 4), lax.rem(i, 4)
                o2[turn, 8 * turn + i] = (chip({A: to[A], B: 2 * turn + b, D: d}) + i1[turn, i].astype(F32)).astype(BF16)

            added = pl.ds(8 * turn, 8)
            wires.go(6 + turn, o2.at[turn, added], i2.at[turn, added], to)

    def r3():
        me = here()
        have(me, 3)
        for turn in (0, 1):
            wires.wait(18 + turn, i2.at[turn, pl.ds(8 * (1 - turn), 8)], me)
            wires.wait(6 + turn, i2.at[turn, pl.ds(8 * turn, 8)], me)

        @pl.loop(0, 16)
        def _(i):
            k1[i] = chip({A: me[A], B: lax.div(i, 4), D: lax.rem(i, 4)}) + i2[0, i].astype(F32) + i2[1, i].astype(F32)

        far = lax.rem(me[B] + 2, 4)
        for turn, step in ((0, 1), (1, 3)):
            for d in range(2):
                o3[turn, d] = k1[far * 4 + 2 * turn + d].astype(BF16)
            wires.go(8 + turn, o3.at[turn], i3.at[turn], moved(me, B, step))

    def r4():
        me = here()
        for turn, step in ((0, 1), (1, 3)):
            wires.wait(8 + turn, i3.at[turn], me)
            to = moved(me, B, step)
            for d in range(2):
                o4[turn, 2 * turn + d] = (k1[to[B] * 4 + 2 * turn + d] + i3[turn, d].astype(F32)).astype(BF16)
                o4[turn, 2 * (1 - turn) + d] = k1[to[B] * 4 + 2 * (1 - turn) + d].astype(BF16)
            wires.go(10 + turn, o4.at[turn], i4.at[turn], to)

    def r5():
        me = here()
        for turn in (0, 1):
            wires.wait(10 + turn, i4.at[turn], me)
        for d in range(4):
            k2[d] = k1[me[B] * 4 + d] + i4[0, d].astype(F32) + i4[1, d].astype(F32)
        for j in (1, 2, 3):
            to = moved(me, D, j)
            o5[j - 1] = k2[to[D]].astype(BF16)
            wires.go(11 + j, o5.at[j - 1], i5.at[j - 1], to)

    def r6():
        me = here()
        total = k2[me[D]]
        for j in (1, 2, 3):
            wires.wait(11 + j, i5.at[j - 1], me)
            total = total + i5[j - 1].astype(F32)
        ob[me["x"]] = total.astype(BF16)
        for j in (1, 2, 3):
            wires.go(14 + j, ob.at[me["x"]], ob.at[me["x"]], moved(me, "x", j))

    def put(q):
        return pltpu.make_async_copy(ob.at[q], out.at[:, pl.ds(q * w, w)], local.at[4 + q])

    def r7():
        me = here()
        for j in (1, 2, 3):
            wires.wait(14 + j, ob.at[moved(me, "x", 4 - j)["x"]], me)
        for q in range(4):
            put(q).start()
        for k in range(4):
            if there is None:
                wires.sent(k, quarter(mates, me, k), me)
        for turn in (0, 1):
            wires.sent(4 + turn, o1.at[turn], me)
            wires.sent(6 + turn, o2.at[turn, pl.ds(8 * turn, 8)], me)
            wires.sent(18 + turn, o2.at[turn, pl.ds(8 * (1 - turn), 8)], me)
            wires.sent(8 + turn, o3.at[turn], me)
            wires.sent(10 + turn, o4.at[turn], me)
        for j in (1, 2, 3):
            wires.sent(11 + j, o5.at[j - 1], me)
            wires.sent(14 + j, ob.at[me["x"]], me)
        for q in range(4):
            put(q).wait()

    return [r0, r1, r2, r3, r4, r5, r6, r7]


def cut(term):
    return term.reshape(4, 4, 2, term.shape[0] // 32, term.shape[1])


class Mates(Exchange):
    peers = (("c", 1),)

    def __init__(self, terms):
        self.operands = [cut(t) for t in terms]
        self.in_specs = [ANY] * len(terms)
        self.out_shape = [jax.ShapeDtypeStruct((4, 4, *t.shape[3:]), BF16) for t in self.operands]
        self.out_specs = [ANY] * len(terms)
        self.scratch = [pltpu.SemaphoreType.DMA((len(terms),))] * 2

    def plan(self, ins, outs, scratch):
        wires = Wires(*scratch)

        def begin():
            mate = moved(here(), "c", 1)
            for n, (term, out) in enumerate(zip(ins, outs, strict=True)):
                wires.go(n, term.at[:, :, mate["c"]], out, mate)

        def end():
            me = here()
            for n, out in enumerate(outs):
                wires.wait(n, out, me)
                wires.sent(n, out, me)

        return [[begin, end]]


MATES_MARKS = {0: [(0, 0)], "end": [(0, 1)]}


class Sum(Exchange):
    peers = SUM_PEERS

    def __init__(self, terms, mates=()):
        self.n = len(terms)
        terms = [cut(t) for t in terms]
        self.operands = [*terms, *mates]
        self.in_specs = [ANY] * len(self.operands)
        self.out_shape = [jax.ShapeDtypeStruct(t.shape[3:], BF16) for t in terms]
        self.out_specs = [ANY] * self.n
        self.scratch = [s for t in terms for s in sum_scratch(*t.shape[3:])]

    def plan(self, ins, outs, scratch):
        theres = list(ins[self.n :]) or [None] * self.n
        return [sum_stages(SUM_ORDERS[i], ins[i], theres[i], outs[i], scratch[SUM_REFS * i : SUM_REFS * (i + 1)]) for i in range(self.n)]


def all_of(*numbers):
    return [(which, number) for number in numbers for which in range(3)]


SUM_LONG_MARKS = {0: all_of(0), 1: all_of(1), 3: all_of(2), 5: all_of(3), 6: all_of(4), 7: all_of(5), 8: all_of(6), "end": all_of(7)}
SUM_SHORT_MARKS = {0: all_of(0), 1: all_of(1), 4: all_of(2), 7: all_of(3), "end": all_of(4, 5, 6, 7)}


def dot(a, b, dims=((1,), (0,))):
    return lax.dot_general(a, b, (dims, ((), ())), preferred_element_type=F32)


def scale_of(wide):
    return lax.rsqrt(jnp.mean(wide * wide, -1, keepdims=True) + 1e-6)


def norm_into(h, a, at, chunk=512):
    @pl.loop(0, h.shape[0], step=chunk)
    def _(m):
        rows = pl.ds(m, chunk)
        wide = h[rows, :].astype(F32)
        value = (wide * scale_of(wide)).astype(BF16)
        if a is not None:
            a[rows, :] = value
        if at is not None:
            at[:, rows] = value.T


def whole(shape):
    return pl.BlockSpec(shape, lambda i: (0,) * len(shape), pipeline_mode=pl.Buffered(1))


TILE, CHUNK = 256, 512


def call(kernel, grid, operands, in_specs, out_shape, out_specs, scratch, name, exchange=None, marks=None, collective_id=None):
    counts = [len(operands), len(out_shape), len(scratch)]
    extra = [exchange.operands, exchange.out_shape, exchange.scratch] if exchange else [[], [], []]
    n_extra = [len(e) for e in extra]

    def body(*refs):
        refs, mine, theirs = list(refs), [], []
        for n, k in zip(counts, n_extra, strict=True):
            mine += refs[:n]
            theirs.append(refs[n : n + k])
            refs = refs[n + k :]
        i = pl.program_id(0)
        if exchange:
            plan = exchange.plan(*theirs)
            exchange.grid_step(plan, marks, i)
        kernel(*mine)
        if exchange:

            @pl.when(i == grid - 1)
            def _():
                exchange.finish(plan, marks)

    params = dict(collective_id=collective_id, has_side_effects=True) if exchange else {}
    out = pl.pallas_call(
        body,
        grid=(grid,),
        out_shape=list(out_shape) + (exchange.out_shape if exchange else []),
        in_specs=list(in_specs) + (exchange.in_specs if exchange else []),
        out_specs=list(out_specs) + (exchange.out_specs if exchange else []),
        scratch_shapes=list(scratch) + (exchange.scratch if exchange else []),
        compiler_params=pltpu.CompilerParams(vmem_limit_bytes=LIMIT, **params),
        name=name,
    )(*operands, *(exchange.operands if exchange else []))
    return out[: counts[1]], out[counts[1] :]


PIECES = ((0, 256, 0), (256, 256, 1), (512, 512, 2), (1024, 512, 4), (1536, 512, 6), (2048, 512, 8))
DOWN_AT = (-4, -2, -1, 0, 1, 5, 7, 9)
NEXT_DOWN_AT = (1, 2, 3, 4, 6, 10, 12, 99)
NEXT_AT = (5, 6, 7, 10, 11, 99)
EARLY = 1024


def forward(h, weights, collective_id):
    tokens, d = h.shape
    ff = weights[0].shape[2]
    tiles, outs = ff // TILE, d // TILE
    steps = tiles + outs
    pieces = len(PIECES)
    now = [jax.ShapeDtypeStruct(w.shape[1:], BF16) for w in weights]
    later = [jax.ShapeDtypeStruct((w.shape[1], EARLY), BF16) for w in weights[:2]] + now[2:]
    next_layer = Gather(later)

    def kernel(h_ref, wg_ref, wu_ref, wd_ref, y_ref, g_ref, u_ref, at_ref, fg, fu, fd, hg, hu, hd, a, act, vg, vu, vd, local, csend, crecv, dsend, drecv, *scratch):
        i = pl.program_id(0)
        ng, nu, nd = wg_ref.at[0], wu_ref.at[0], wd_ref.at[0]
        lg, lu, ld = wg_ref.at[1, :, pl.ds(0, EARLY)], wu_ref.at[1, :, pl.ds(0, EARLY)], wd_ref.at[1]
        todo = {}

        def plan(at, stages):
            for k, stage in zip(at, stages):
                todo.setdefault(min(k, steps), []).append(stage)

        def keep(n, src, dst):
            return pltpu.make_async_copy(src, dst, local.at[2 * pieces + 1 + n])

        matrices = ((("z", "y"), ng, vg), (("y", "z"), nu, vu))
        for k in reversed(range(pieces)):
            start, size, need = PIECES[k]
            for m, (order, w, full) in enumerate(matrices):
                n = m * pieces + k
                if k == 0:
                    plan((-4, -1, 0, 99), gather_stages_direct(w, full, local.at[n], dsend.at[m], drecv.at[m], start, size))
                else:
                    plan((*range(need - 4, need + 1), 99), gather_stages_chunk(*order, w, full, local.at[n], csend.at[n], crecv.at[n], start, size))
        plan(DOWN_AT, gather_stages_x("z", "y", nd, vd, local.at[2 * pieces], dsend.at[2], drecv.at[2]))
        plan((tiles, tiles, tiles, 99, 99, 99), [keep(0, vg, fg).start, keep(1, vu, fu).start, keep(2, vd, fd).start, keep(0, vg, fg).wait, keep(1, vu, fu).wait, keep(2, vd, fd).wait])
        after = next_layer.plan((lg, lu, ld), (hg, hu, hd), scratch)
        for which, at in enumerate((NEXT_AT, NEXT_AT, NEXT_DOWN_AT)):
            plan(at, after[which])

        @pl.when(i == 0)
        def _():
            greet(PLANE_PEERS)
            for t in sorted(todo):
                if t < 0:
                    for f in todo[t]:
                        f()
                if t == -3:
                    norm_into(h_ref, a, at_ref)

        for at in range(steps):
            if at in todo:

                @pl.when(i == at)
                def _():
                    for f in todo[at]:
                        f()

        @pl.when(i < tiles)
        def _():
            cols = pl.ds(pl.multiple_of(i * TILE, TILE), TILE)
            wg = vg[:, :, :, :, cols].reshape(d, TILE)
            wu = vu[:, :, :, :, cols].reshape(d, TILE)

            @pl.loop(0, tokens, step=CHUNK)
            def _(m):
                rows = pl.ds(m, CHUNK)
                g = dot(a[rows, :], wg)
                u = dot(a[rows, :], wu)
                g_ref[rows, :] = g
                u_ref[rows, :] = u
                act[i, rows, :] = (g * jax.nn.sigmoid(g) * u).astype(BF16)

        @pl.when(i >= tiles)
        def _():
            cols = pl.ds(pl.multiple_of((i - tiles) * TILE, TILE), TILE)

            @pl.loop(0, tokens, step=CHUNK)
            def _(m):
                rows = pl.ds(m, CHUNK)
                total = sum(dot(act[k, rows, :], vd[:, :, :, :, cols].reshape(ff, TILE)[k * TILE : (k + 1) * TILE, :]) for k in range(tiles))
                y_ref[rows, :] = h_ref[rows, cols] + total.astype(BF16)

        @pl.when(i == steps - 1)
        def _():
            for f in todo[steps]:
                f()

    tile = pl.BlockSpec((tokens, TILE), lambda i: (0, jnp.minimum(i, tiles - 1)))
    full_types = [jax.ShapeDtypeStruct(blocks_of(w), BF16) for w in (*now, *later)]
    dma = pltpu.SemaphoreType.DMA
    out = pl.pallas_call(
        kernel,
        grid=(steps,),
        out_shape=[
            jax.ShapeDtypeStruct(h.shape, BF16),
            jax.ShapeDtypeStruct((tokens, ff), F32),
            jax.ShapeDtypeStruct((tokens, ff), F32),
            jax.ShapeDtypeStruct((d, tokens), BF16),
            *full_types,
        ],
        in_specs=[whole(h.shape)] + [whole(w.shape) for w in weights],
        out_specs=[pl.BlockSpec((tokens, TILE), lambda i: (0, jnp.maximum(i - tiles, 0))), tile, tile, whole((d, tokens))] + [ANY] * 6,
        scratch_shapes=[
            pltpu.VMEM(h.shape, BF16),
            pltpu.VMEM((tiles, tokens, TILE), BF16),
            *(pltpu.VMEM(t.shape, BF16) for t in full_types[:3]),
            dma((2 * pieces + 4,)),
            dma((2 * pieces, 8)),
            dma((2 * pieces, 8)),
            dma((3, 16)),
            dma((3, 16)),
            *next_layer.scratch,
        ],
        compiler_params=pltpu.CompilerParams(vmem_limit_bytes=LIMIT, collective_id=collective_id, has_side_effects=True),
        name="forward",
    )(h, *weights)
    return out[:4], [f.reshape(-1, f.shape[-1]) for f in out[4:]]


def hidden_grads(g, u, by_act):
    sig = jax.nn.sigmoid(g)
    silu = g * sig
    by_act = by_act.astype(BF16).astype(F32)
    return (silu * u).astype(BF16), (by_act * u * (sig * (1 + g * (1 - sig)))).astype(BF16), (by_act * silu).astype(BF16)


def backward_fresh(h, by_y, early, weights, wd, collective_id):
    tokens, d = h.shape
    ff = wd.shape[0]
    steps, first = ff // TILE, EARLY // TILE
    late = ff - EARLY

    def kernel(h_ref, ga, ua, wg_ref, wu_ref, by_ref, wd_ref, dg_ref, du_ref, dwg_ref, dwu_ref, dwd_ref, hg, hu, a, at, act, tg, tu, vg, vu, local, send, recv):
        i = pl.program_id(0)
        lists = [
            gather_stages_chunk(*order, w.at[1], full, local.at[n], send.at[n], recv.at[n], EARLY, late, 0)
            for n, (order, w, full) in enumerate(((("z", "y"), wg_ref, vg), (("y", "z"), wu_ref, vu)))
        ]
        keep = [pltpu.make_async_copy(v, o, local.at[2 + n]) for n, (v, o) in enumerate(((vg, hg), (vu, hu)))]

        for at_step in range(first + 1):

            @pl.when(i == at_step)
            def _():
                if at_step == 0:
                    greet(Gather.peers)
                for stages in lists:
                    stages[at_step]()
                if at_step == 0:
                    norm_into(h_ref, a, at)
                if at_step == first:
                    for k in keep:
                        k.start()

        @pl.when(i < first)
        def _():
            cols = pl.ds(pl.multiple_of(i * TILE, TILE), TILE)
            tg[...] = ga[:, cols]
            tu[...] = ua[:, cols]

        @pl.when(i >= first)
        def _():
            cols = pl.ds(pl.multiple_of((i - first) * TILE, TILE), TILE)
            tg[...] = vg[:, :, :, :, cols].reshape(d, TILE)
            tu[...] = vu[:, :, :, :, cols].reshape(d, TILE)

        @pl.loop(0, tokens, step=CHUNK)
        def _(m):
            rows = pl.ds(m, CHUNK)
            g, u = dot(a[rows, :], tg[...]), dot(a[rows, :], tu[...])
            by_act = dot(by_ref[rows, :], wd_ref[...], ((1,), (1,)))
            act[rows, :], dg_ref[rows, :], du_ref[rows, :] = hidden_grads(g, u, by_act)

        dwd_ref[...] = dot(act[...], by_ref[...], ((0,), (0,))).astype(BF16)
        dwg_ref[...] = dot(at[...], dg_ref[...]).astype(BF16)
        dwu_ref[...] = dot(at[...], du_ref[...]).astype(BF16)

        @pl.when(i == steps - 1)
        def _():
            for stages in lists:
                stages[5]()
            for k in keep:
                k.wait()

    across = pl.BlockSpec((d, TILE), lambda i: (0, i))
    down = pl.BlockSpec((TILE, d), lambda i: (i, 0))
    tile = pl.BlockSpec((tokens, TILE), lambda i: (0, i))
    part = (4, 4, 2, d // 32, late)
    dma = pltpu.SemaphoreType.DMA
    out = pl.pallas_call(
        kernel,
        grid=(steps,),
        out_shape=[jax.ShapeDtypeStruct((tokens, ff), BF16)] * 2
        + [jax.ShapeDtypeStruct((d, ff), BF16)] * 2
        + [jax.ShapeDtypeStruct((ff, d), BF16)]
        + [jax.ShapeDtypeStruct(part, BF16)] * 2,
        in_specs=[whole((tokens, d)), *[whole((d, EARLY))] * 2, *[whole(w.shape) for w in weights[:2]], whole((tokens, d)), down],
        out_specs=[tile, tile, across, across, down, ANY, ANY],
        scratch_shapes=[
            pltpu.VMEM((tokens, d), BF16),
            pltpu.VMEM((d, tokens), BF16),
            pltpu.VMEM((tokens, TILE), BF16),
            *[pltpu.VMEM((d, TILE), BF16)] * 2,
            *[pltpu.VMEM(part, BF16)] * 2,
            dma((4,)),
            dma((2, 8)),
            dma((2, 8)),
        ],
        compiler_params=pltpu.CompilerParams(vmem_limit_bytes=LIMIT, collective_id=collective_id, has_side_effects=True),
        name="backward_fresh",
    )(h, *early, *weights[:2], by_y, wd)
    return out[:2], out[2:5], [f.reshape(d, late) for f in out[5:]]


def backward_hidden(by_y, wd, saved, **beside):
    tokens, d = by_y.shape
    ff = wd.shape[0]
    steps = ff // TILE

    def kernel(at, g_ref, u_ref, by_ref, wd_ref, dg_ref, du_ref, dwg_ref, dwu_ref, dwd_ref, act):
        @pl.loop(0, tokens, step=CHUNK)
        def _(m):
            rows = pl.ds(m, CHUNK)
            by_act = dot(by_ref[rows, :], wd_ref[...], ((1,), (1,)))
            act[rows, :], dg_ref[rows, :], du_ref[rows, :] = hidden_grads(g_ref[rows, :], u_ref[rows, :], by_act)

        dwd_ref[...] = dot(act[...], by_ref[...], ((0,), (0,))).astype(BF16)
        dwg_ref[...] = dot(at[...], dg_ref[...]).astype(BF16)
        dwu_ref[...] = dot(at[...], du_ref[...]).astype(BF16)

    across = pl.BlockSpec((d, TILE), lambda i: (0, i))
    down = pl.BlockSpec((TILE, d), lambda i: (i, 0))
    tile = pl.BlockSpec((tokens, TILE), lambda i: (0, i))
    return call(
        kernel,
        steps,
        (*saved, by_y, wd),
        [whole((d, tokens)), tile, tile, whole((tokens, d)), down],
        [jax.ShapeDtypeStruct((tokens, ff), BF16)] * 2 + [jax.ShapeDtypeStruct((d, ff), BF16)] * 2 + [jax.ShapeDtypeStruct((ff, d), BF16)],
        [tile, tile, across, across, down],
        [pltpu.VMEM((tokens, TILE), BF16)],
        "backward_hidden",
        **beside,
    )


def backward_input(dg, du, wgs, wus, h, by_y, **beside):
    tokens, d = h.shape
    ff = dg.shape[1]
    chunk = 256

    n = len(wgs)

    def kernel(dg_ref, du_ref, *refs):
        parts, (h_ref, by_ref, out_ref) = refs[: 2 * n], refs[2 * n :]
        by_a, start = 0, 0
        for wg_ref, wu_ref in zip(parts[:n], parts[n:], strict=True):
            cols = pl.ds(start, wg_ref.shape[1])
            start += wg_ref.shape[1]
            by_a = by_a + dot(dg_ref[:, cols], wg_ref[...], ((1,), (1,))) + dot(du_ref[:, cols], wu_ref[...], ((1,), (1,)))
        by_a = by_a.astype(BF16).astype(F32)
        wide = h_ref[...].astype(F32)
        scale = scale_of(wide)
        back = jnp.sum(by_a * wide, -1, keepdims=True) * (scale * scale * scale) * (1 / d)
        out_ref[...] = by_ref[...] + (by_a * scale - wide * back).astype(BF16)

    rows = lambda n: pl.BlockSpec((chunk, n), lambda i: (i, 0))
    return call(
        kernel,
        tokens // chunk,
        (dg, du, *wgs, *wus, h, by_y),
        [rows(ff), rows(ff), *(whole(w.shape) for w in (*wgs, *wus)), rows(d), rows(d)],
        [jax.ShapeDtypeStruct(h.shape, BF16)],
        [rows(d)],
        [],
        "backward_input",
        **beside,
    )


def stacked(layers):
    n = len(layers[0])

    def kernel(*refs):
        for k in range(n):
            for layer in range(len(layers)):
                refs[len(layers) * n + k][layer] = refs[layer * n + k][...]

    return pl.pallas_call(
        kernel,
        out_shape=[jax.ShapeDtypeStruct((len(layers), *t.shape), BF16) for t in layers[0]],
        name="stacked",
    )(*(t for layer in layers for t in layer))


def solution(mesh):
    def step(x, dy, *weights):
        x, dy = x[0], dy[0]
        (h1, g0, u0, at0), (wg0, wu0, wd0, wg1, wu1, wd1) = forward(x, weights, 1)
        (dg1, du1), terms1, (wg1_rest, wu1_rest) = backward_fresh(h1, dy, (wg1, wu1), weights, wd1, 2)
        (by_h1,), mates1 = backward_input(dg1, du1, (wg1, wg1_rest), (wu1, wu1_rest), h1, dy, exchange=Mates(terms1), marks=MATES_MARKS, collective_id=3)
        (dg0, du0, *terms0), sums1 = backward_hidden(by_h1, wd0, (at0, g0, u0), exchange=Sum(terms1, mates1), marks=SUM_LONG_MARKS, collective_id=4)
        (by_x,), sums0 = backward_input(dg0, du0, (wg0,), (wu0,), x, by_h1, exchange=Sum(terms0), marks=SUM_SHORT_MARKS, collective_id=5)
        return (by_x[None], *stacked([sums0, sums1]))

    states, shard = P(("rep", "r", "s"), None, None), P(None, "s", None)
    return jax.shard_map(
        step,
        mesh=mesh,
        in_specs=(states, states) + (shard,) * 3,
        out_specs=(states,) + (P("rep", "s", None),) * 3,
        check_vma=False,
    )
```

time: 520 us -> 371 us (0.71)
  Pallas kernels: 510 us -> 366 us
    pallas_call x8 -> x5, Pallas kernels: 459 us -> 267 us  [the longest x3 173 us: call(): pl.pallas_call(body, grid=(grid,), out_shape=list(out_shape) + (exchange....]
    pallas_call x1, Pallas kernels: 51 us -> 98.9 us  [forward(): pl.pallas_call(kernel, grid=(steps,), out_shape=[jax.ShapeDtypeStruct(h.s...]
where the time goes in v2:
time: 371 us
  Pallas kernels  366 us (99%)
  local copies, waits for them, and re-layouts  4.64 us (1%)
    pallas_call x3, Pallas kernels, call(): pl.pallas_call(body, grid=(grid,), out_shape=list(out_shape) + (exchange....  173 us
    pallas_call x1, Pallas kernels, forward(): pl.pallas_call(kernel, grid=(steps,), out_shape=[jax.ShapeDtypeStruct(h.s...  98.9 us
    pallas_call x1, Pallas kernels, backward_fresh(): pl.pallas_call(kernel, grid=(steps,), out_shape=[jax.ShapeDtypeStruct((to...  91.9 us

profile of v2, /device:TPU:0, one launch (start us, length us, event | category | flops | bytes accessed | tf_op | source)
XLA Modules:
  0.0 371.0 jit_solution(8674823793694978264)
XLA Ops:
  0.6 98.9 %forward.1 = (bf16[2048,1024]{1,0:T(8,128)(2,1)}, f32[2048,2560]{1,0:T(8,128)}, f32[2048,2560]{1,0:T(8,128)}, bf16[1024,2048]{1,0:T(8,128)(2,1)}, bf16[4,4,2,32,...) custom-call(bf16[2048,1024]{1,0:T(8,128)(2,1)} %bitcast.23, ...), custom_call_target="tpu_custom_call" | custom-call | tf_op jit(solution)/shard_map/forward/pallas_call | solution.py:774
  99.5 91.9 %backward_fresh.1 = (bf16[2048,2560]{1,0:T(8,128)(2,1)}, bf16[2048,2560]{1,0:T(8,128)(2,1)}, bf16[1024,2560]{1,0:T(8,128)(2,1)}, bf16[1024,2560]{1,0:T(8,128)(2,...) custom-call(bf16[2048,1024]{1,0:T(8,128)(2,1)} %get-tuple-element.43.h_re, ...), custom_call_target="tpu_custom_call" | custom-call | tf_op jit(solution)/shard_map/backward_fresh/pallas_call | solution.py:873
  191.4 31.4 %backward_input.2 = (bf16[2048,1024]{1,0:T(8,128)(2,1)}, bf16[4,4,32,2560]{3,2,1,0:T(8,128)(2,1)}, bf16[4,4,32,2560]{3,2,1,0:T(8,128)(2,1)}, bf16[4,4,80,1024]{3,2,1,0:T(8,128)(2,1)}) custom-call(bf16[2048,2560]{1,0:T(8,128)(2,1)} %get-tuple-element.47.refs_0_, bf16[2048,2560]{1,0:T(8,128)(2,1)} %get-tuple-element.48.refs_1_, bf16[1024,1024]{1,0:T(8,128)(2,1)} %bitcast.28, ...), custom_call_target="tpu_custom_call" | custom-call | tf_op jit(solution)/shard_map/backward_input/pallas_call | solution.py:665
  222.8 77.3 %backward_hidden.1 = (bf16[2048,2560]{1,0:T(8,128)(2,1)}, bf16[2048,2560]{1,0:T(8,128)(2,1)}, bf16[1024,2560]{1,0:T(8,128)(2,1)}, bf16[1024,2560]{1,0:T(8,128)(2...) custom-call(bf16[1024,2048]{1,0:T(8,128)(2,1)} %get-tuple-element.40, ...), custom_call_target="tpu_custom_call" | custom-call | tf_op jit(solution)/shard_map/backward_hidden/pallas_call | solution.py:665
  300.1 64.0 %backward_input.3 = (bf16[2048,1024]{1,0:T(8,128)(2,1)}, bf16[32,2560]{1,0:T(8,128)(2,1)}, bf16[32,2560]{1,0:T(8,128)(2,1)}, bf16[80,1024]{1,0:T(8,128)(2,1)}) custom-call(bf16[2048,2560]{1,0:T(8,128)(2,1)} %get-tuple-element.59.refs_0_, bf16[2048,2560]{1,0:T(8,128)(2,1)} %get-tuple-element.60.refs_1_, bf16[1024,2560]{1,0:T(8,128)(2,1)} %bitcast.33, ...), custom_call_target="tpu_custom_call" | custom-call | tf_op jit(solution)/shard_map/backward_input/pallas_call | solution.py:665
  364.1 2.3 stacked.1
  366.3 4.6 %copy.10 = bf16[1,2048,1024]{2,1,0:T(8,128)(2,1)} copy(bf16[1,2048,1024]{2,1,0:T(8,128)(2,1)} %bitcast.38) | data formatting | bytes 8388608

commit v3 on v2

--- a/solution.py
+++ b/solution.py
@@ -608,8 +608,8 @@
     return [(which, number) for number in numbers for which in range(3)]
 
 
-SUM_LONG_MARKS = {0: all_of(0), 1: all_of(1), 3: all_of(2), 5: all_of(3), 6: all_of(4), 7: all_of(5), 8: all_of(6), "end": all_of(7)}
-SUM_SHORT_MARKS = {0: all_of(0), 1: all_of(1), 4: all_of(2), 7: all_of(3), "end": all_of(4, 5, 6, 7)}
+SUM_LONG_MARKS = {0: all_of(0), 1: all_of(1), 3: all_of(2), 6: all_of(3), 7: all_of(4), 8: all_of(5), 9: all_of(6), "end": all_of(7)}
+SUM_SHORT_MARKS = {0: all_of(0, 1), 3: all_of(2), 6: all_of(3), 7: all_of(4), "end": all_of(5, 6, 7)}
 
 
 def dot(a, b, dims=((1,), (0,))):
@@ -636,7 +636,7 @@
     return pl.BlockSpec(shape, lambda i: (0,) * len(shape), pipeline_mode=pl.Buffered(1))
 
 
-TILE, CHUNK = 256, 512
+TILE, CHUNK, CHUNK_FRESH, CHUNK_HIDDEN = 256, 512, 1024, 256
 
 
 def call(kernel, grid, operands, in_specs, out_shape, out_specs, scratch, name, exchange=None, marks=None, collective_id=None):
@@ -676,6 +676,7 @@
 
 
 PIECES = ((0, 256, 0), (256, 256, 1), (512, 512, 2), (1024, 512, 4), (1536, 512, 6), (2048, 512, 8))
+PIECES_AT = ((-4, -1, 0, 99), (-3, -2, -1, 0, 1, 99), (-2, -1, 0, 1, 2, 99), (0, 1, 2, 3, 4, 99), (2, 3, 4, 5, 6, 99), (4, 5, 6, 7, 8, 99))
 DOWN_AT = (-4, -2, -1, 0, 1, 5, 7, 9)
 NEXT_DOWN_AT = (1, 2, 3, 4, 6, 10, 12, 99)
 NEXT_AT = (5, 6, 7, 10, 11, 99)
@@ -707,13 +708,13 @@
 
         matrices = ((("z", "y"), ng, vg), (("y", "z"), nu, vu))
         for k in reversed(range(pieces)):
-            start, size, need = PIECES[k]
+            start, size, _ = PIECES[k]
             for m, (order, w, full) in enumerate(matrices):
                 n = m * pieces + k
                 if k == 0:
-                    plan((-4, -1, 0, 99), gather_stages_direct(w, full, local.at[n], dsend.at[m], drecv.at[m], start, size))
+                    plan(PIECES_AT[k], gather_stages_direct(w, full, local.at[n], dsend.at[m], drecv.at[m], start, size))
                 else:
-                    plan((*range(need - 4, need + 1), 99), gather_stages_chunk(*order, w, full, local.at[n], csend.at[n], crecv.at[n], start, size))
+                    plan(PIECES_AT[k], gather_stages_chunk(*order, w, full, local.at[n], csend.at[n], crecv.at[n], start, size))
         plan(DOWN_AT, gather_stages_x("z", "y", nd, vd, local.at[2 * pieces], dsend.at[2], drecv.at[2]))
         plan((tiles, tiles, tiles, 99, 99, 99), [keep(0, vg, fg).start, keep(1, vu, fu).start, keep(2, vd, fd).start, keep(0, vg, fg).wait, keep(1, vu, fu).wait, keep(2, vd, fd).wait])
         after = next_layer.plan((lg, lu, ld), (hg, hu, hd), scratch)
@@ -744,7 +745,7 @@
             wg = vg[:, :, :, :, cols].reshape(d, TILE)
             wu = vu[:, :, :, :, cols].reshape(d, TILE)
 
-            @pl.loop(0, tokens, step=CHUNK)
+            @pl.loop(0, tokens, step=CHUNK, unroll=True)
             def _(m):
                 rows = pl.ds(m, CHUNK)
                 g = dot(a[rows, :], wg)
@@ -757,7 +758,7 @@
         def _():
             cols = pl.ds(pl.multiple_of((i - tiles) * TILE, TILE), TILE)
 
-            @pl.loop(0, tokens, step=CHUNK)
+            @pl.loop(0, tokens, step=CHUNK, unroll=True)
             def _(m):
                 rows = pl.ds(m, CHUNK)
                 total = sum(dot(act[k, rows, :], vd[:, :, :, :, cols].reshape(ff, TILE)[k * TILE : (k + 1) * TILE, :]) for k in range(tiles))
@@ -847,9 +848,9 @@
             tg[...] = vg[:, :, :, :, cols].reshape(d, TILE)
             tu[...] = vu[:, :, :, :, cols].reshape(d, TILE)
 
-        @pl.loop(0, tokens, step=CHUNK)
+        @pl.loop(0, tokens, step=CHUNK_FRESH, unroll=True)
         def _(m):
-            rows = pl.ds(m, CHUNK)
+            rows = pl.ds(m, CHUNK_FRESH)
             g, u = dot(a[rows, :], tg[...]), dot(a[rows, :], tu[...])
             by_act = dot(by_ref[rows, :], wd_ref[...], ((1,), (1,)))
             act[rows, :], dg_ref[rows, :], du_ref[rows, :] = hidden_grads(g, u, by_act)
@@ -901,9 +902,9 @@
     steps = ff // TILE
 
     def kernel(at, g_ref, u_ref, by_ref, wd_ref, dg_ref, du_ref, dwg_ref, dwu_ref, dwd_ref, act):
-        @pl.loop(0, tokens, step=CHUNK)
+        @pl.loop(0, tokens, step=CHUNK_HIDDEN, unroll=True)
         def _(m):
-            rows = pl.ds(m, CHUNK)
+            rows = pl.ds(m, CHUNK_HIDDEN)
             by_act = dot(by_ref[rows, :], wd_ref[...], ((1,), (1,)))
             act[rows, :], dg_ref[rows, :], du_ref[rows, :] = hidden_grads(g_ref[rows, :], u_ref[rows, :], by_act)
 
@@ -961,19 +962,30 @@
     )
 
 
-def stacked(layers):
-    n = len(layers[0])
-
-    def kernel(*refs):
-        for k in range(n):
-            for layer in range(len(layers)):
-                refs[len(layers) * n + k][layer] = refs[layer * n + k][...]
-
+def results(by_x, layers):
+    n, tokens = len(layers[0]), by_x.shape[0]
+    steps = 4
+
+    def kernel(x_ref, *refs):
+        out_ref, outs = refs[len(layers) * n], refs[len(layers) * n + 1 :]
+        out_ref[...] = x_ref[...]
+
+        @pl.when(pl.program_id(0) == 0)
+        def _():
+            for k in range(n):
+                for layer in range(len(layers)):
+                    outs[k][layer] = refs[layer * n + k][...]
+
+    rows = pl.BlockSpec((tokens // steps, by_x.shape[1]), lambda i: (i, 0))
+    shapes = [(len(layers), *t.shape) for t in layers[0]]
     return pl.pallas_call(
         kernel,
-        out_shape=[jax.ShapeDtypeStruct((len(layers), *t.shape), BF16) for t in layers[0]],
-        name="stacked",
-    )(*(t for layer in layers for t in layer))
+        grid=(steps,),
+        out_shape=[jax.ShapeDtypeStruct(by_x.shape, BF16)] + [jax.ShapeDtypeStruct(shape, BF16) for shape in shapes],
+        in_specs=[rows] + [whole(t.shape) for layer in layers for t in layer],
+        out_specs=[rows] + [whole(shape) for shape in shapes],
+        name="results",
+    )(by_x, *(t for layer in layers for t in layer))
 
 
 def solution(mesh):
@@ -984,7 +996,8 @@
         (by_h1,), mates1 = backward_input(dg1, du1, (wg1, wg1_rest), (wu1, wu1_rest), h1, dy, exchange=Mates(terms1), marks=MATES_MARKS, collective_id=3)
         (dg0, du0, *terms0), sums1 = backward_hidden(by_h1, wd0, (at0, g0, u0), exchange=Sum(terms1, mates1), marks=SUM_LONG_MARKS, collective_id=4)
         (by_x,), sums0 = backward_input(dg0, du0, (wg0,), (wu0,), x, by_h1, exchange=Sum(terms0), marks=SUM_SHORT_MARKS, collective_id=5)
-        return (by_x[None], *stacked([sums0, sums1]))
+        by_x, *by_weights = results(by_x, [sums0, sums1])
+        return (by_x[None], *by_weights)
 
     states, shard = P(("rep", "r", "s"), None, None), P(None, "s", None)
     return jax.shard_map(

time: 371 us -> 357 us (0.962)
  Pallas kernels: 366 us -> 356 us
  local copies, waits for them, and re-layouts: 4.64 us -> 0 us
    pallas_call x1, Pallas kernels: 91.9 us -> 86.2 us  [backward_fresh(): pl.pallas_call(kernel, grid=(steps,), out_shape=[jax.ShapeDtypeStruct((to...]
    unnamed x1 -> x0, local copies, waits for them, and re-layouts: 4.64 us -> none
    pallas_call x3, Pallas kernels: 173 us -> 168 us  [call(): pl.pallas_call(body, grid=(grid,), out_shape=list(out_shape) + (exchange....]
where the time goes in v3:
time: 357 us
  Pallas kernels  356 us (100%)
    pallas_call x3, Pallas kernels, call(): pl.pallas_call(body, grid=(grid,), out_shape=list(out_shape) + (exchange....  168 us
    pallas_call x1, Pallas kernels, forward(): pl.pallas_call(kernel, grid=(steps,), out_shape=[jax.ShapeDtypeStruct(h.s...  96.3 us
    pallas_call x1, Pallas kernels, backward_fresh(): pl.pallas_call(kernel, grid=(steps,), out_shape=[jax.ShapeDtypeStruct((to...  86.2 us

profile of v3, /device:TPU:0, one launch (start us, length us, event | category | flops | bytes accessed | tf_op | source)
XLA Modules:
  0.0 356.8 jit_solution(1843102557451067984)
XLA Ops:
  0.6 96.3 %forward.1 = (bf16[2048,1024]{1,0:T(8,128)(2,1)}, f32[2048,2560]{1,0:T(8,128)}, f32[2048,2560]{1,0:T(8,128)}, bf16[1024,2048]{1,0:T(8,128)(2,1)}, bf16[4,4,2,32,...) custom-call(bf16[2048,1024]{1,0:T(8,128)(2,1)} %bitcast.23, ...), custom_call_target="tpu_custom_call" | custom-call | tf_op jit(solution)/shard_map/forward/pallas_call | solution.py:775
  97.0 86.2 %backward_fresh.1 = (bf16[2048,2560]{1,0:T(8,128)(2,1)}, bf16[2048,2560]{1,0:T(8,128)(2,1)}, bf16[1024,2560]{1,0:T(8,128)(2,1)}, bf16[1024,2560]{1,0:T(8,128)(2,...) custom-call(bf16[2048,1024]{1,0:T(8,128)(2,1)} %get-tuple-element.44.h_re, ...), custom_call_target="tpu_custom_call" | custom-call | tf_op jit(solution)/shard_map/backward_fresh/pallas_call | solution.py:874
  183.2 31.4 %backward_input.2 = (bf16[2048,1024]{1,0:T(8,128)(2,1)}, bf16[4,4,32,2560]{3,2,1,0:T(8,128)(2,1)}, bf16[4,4,32,2560]{3,2,1,0:T(8,128)(2,1)}, bf16[4,4,80,1024]{3,2,1,0:T(8,128)(2,1)}) custom-call(bf16[2048,2560]{1,0:T(8,128)(2,1)} %get-tuple-element.48.refs_0_, bf16[2048,2560]{1,0:T(8,128)(2,1)} %get-tuple-element.49.refs_1_, bf16[1024,1024]{1,0:T(8,128)(2,1)} %bitcast.28, ...), custom_call_target="tpu_custom_call" | custom-call | tf_op jit(solution)/shard_map/backward_input/pallas_call | solution.py:665
  214.6 72.1 %backward_hidden.1 = (bf16[2048,2560]{1,0:T(8,128)(2,1)}, bf16[2048,2560]{1,0:T(8,128)(2,1)}, bf16[1024,2560]{1,0:T(8,128)(2,1)}, bf16[1024,2560]{1,0:T(8,128)(2...) custom-call(bf16[1024,2048]{1,0:T(8,128)(2,1)} %get-tuple-element.41, ...), custom_call_target="tpu_custom_call" | custom-call | tf_op jit(solution)/shard_map/backward_hidden/pallas_call | solution.py:665
  286.7 64.6 %backward_input.3 = (bf16[2048,1024]{1,0:T(8,128)(2,1)}, bf16[32,2560]{1,0:T(8,128)(2,1)}, bf16[32,2560]{1,0:T(8,128)(2,1)}, bf16[80,1024]{1,0:T(8,128)(2,1)}) custom-call(bf16[2048,2560]{1,0:T(8,128)(2,1)} %get-tuple-element.60.refs_0_, bf16[2048,2560]{1,0:T(8,128)(2,1)} %get-tuple-element.61.refs_1_, bf16[1024,2560]{1,0:T(8,128)(2,1)} %bitcast.33, ...), custom_call_target="tpu_custom_call" | custom-call | tf_op jit(solution)/shard_map/backward_input/pallas_call | solution.py:665
  351.3 5.4 %results.1 = (bf16[2048,1024]{1,0:T(8,128)(2,1)}, bf16[2,32,2560]{2,1,0:T(8,128)(2,1)}, bf16[2,32,2560]{2,1,0:T(8,128)(2,1)}, bf16[2,80,1024]{2,1,0:T(8,128)(2,1)}) custom-call(bf16[2048,1024]{1,0:T(8,128)(2,1)} %get-tuple-element.67.x_ref, bf16[32,2560]{1,0:T(8,128)(2,1)} %get-tuple-element.68.refs_0_, bf16[32,2560]{1,0:T(8,128)(2,1)} %get-tuple-element.69.refs_1_, ...), custom_call_target="tpu_custom_call" | custom-call | tf_op jit(solution)/shard_map/results/pallas_call | solution.py:981
